TPU v7x, 128 devices: a whole 4x4x4 slice. The times are simulated.
128 devices in a mesh: grp: 32 (over z, y, core), mem: 4 (over x).
Axes of the slice: x: 4, y: 4, z: 4, core: 2. Of those that a mesh axis runs over, the one named last changes fastest.
Arguments:
- tiles: bfloat16 [768, 11, 256, 256], P(('grp', 'mem')), as said below
- mask: int32 [768, 11], P(('grp', 'mem')), may hold values from 0 to 1, as said below
- branch: int32 [768], P(('grp', 'mem')), may hold values from 0 to 1
Outputs:
- new_tiles: float32 [768, 11, 256, 256], P(('grp', 'mem'))
- traces: float32 [2], replicated
Inputs may be any that keep to these rules, and one draw needn't show every extreme that they name: X is symmetric: for |d| <= 5, wherever rows i and i + d both lie in the matrix, tiles[i + d, 5 - d] is exactly the transpose of tiles[i, 5 + d]. mask is symmetric in the same way (mask[i + d, 5 - d] == mask[i, 5 + d]); the diagonal slot mask[i, 5] is always 1; slots whose column i - 5 + s lies outside the matrix are 0.
All inputs are finite; a program needn't handle non-finite values.
Results may differ from a plain program's by a relative error of at most 0.0003.
Values may be sent and summed in bfloat16 or wider, within the bound.
No kernel may reach another device: no remote copies, remote signals or barrier semaphores. Data moves between devices by JAX's collectives and lax.ppermute only.
A program may use at most 256 MiB of HBM per device.

v0:
```python
import jax
import jax.numpy as jnp
from jax import lax
from jax.sharding import Mesh
from jax.sharding import PartitionSpec as P

GRP_MEM = ("grp_0", "grp_1", "grp_2", "mem")
GRP = ("grp_0", "grp_1", "grp_2")


def from_behind(value, axis, steps):
    count = lax.axis_size(axis)
    first, last = (max(0, -steps), min(count, count - steps))
    return lax.ppermute(value, axis, [(source, source + steps) for source in range(first, last)])


def by_axis(array, axes):
    for axis in axes:
        array = lax.psum(array, axis)
    return array


def band_square(extended, row_count, half_band, slot_count):
    total = jnp.zeros((row_count, slot_count) + extended.shape[2:], jnp.float32)
    for through in range(slot_count):
        first_slot = max(0, half_band - through)
        last_slot = min(slot_count, slot_count + half_band - through)
        left_tile = extended[half_band : half_band + row_count, through]
        right_tiles = extended[through : through + row_count, first_slot:last_slot]
        product = jnp.einsum(
            "rab,rqbc->rqac", left_tile, right_tiles, preferred_element_type=jnp.float32
        )
        low_out = first_slot + through - half_band
        high_out = last_slot + through - half_band
        total = total.at[:, low_out:high_out].add(product)
    return total


def with_corners(masked, row_count, half_band, slot_count):
    top_corner = jnp.stack(
        [
            masked[row_count - half_band + offset, half_band - offset : 2 * half_band - offset]
            for offset in range(half_band)
        ],
        axis=0,
    )
    bottom_corner = jnp.stack(
        [
            masked[offset, half_band - offset : 2 * half_band - offset]
            for offset in range(half_band)
        ],
        axis=0,
    )
    from_above = from_behind(top_corner, GRP_MEM, 1)
    from_below = from_behind(bottom_corner, GRP_MEM, -1)
    blank = jnp.zeros(masked.shape[2:], masked.dtype)
    upper_rows = []
    lower_rows = []
    for offset in range(half_band):
        upper_slots = []
        lower_slots = []
        for column in range(slot_count):
            across = offset + column - half_band
            if 0 <= across < half_band:
                upper_slots.append(from_above[offset, across])
                lower_slots.append(from_below[offset, across])
            elif across >= half_band:
                upper_slots.append(masked[across - half_band, 2 * half_band - column].T)
                lower_slots.append(blank)
            else:
                upper_slots.append(blank)
                lower_slots.append(masked[row_count + across, 2 * half_band - column].T)
        upper_rows.append(jnp.stack(upper_slots, axis=0))
        lower_rows.append(jnp.stack(lower_slots, axis=0))
    return jnp.concatenate(
        [jnp.stack(upper_rows, axis=0), masked, jnp.stack(lower_rows, axis=0)], axis=0
    )


def on_device(tiles, mask, branch):
    row_count = tiles.shape[0]
    slot_count = tiles.shape[1]
    half_band = (slot_count - 1) // 2
    occupied = mask[:, :, None, None]
    masked = tiles * occupied.astype(tiles.dtype)
    selector = branch[:, None, None, None]
    extended = with_corners(masked, row_count, half_band, slot_count)
    square = band_square(extended, row_count, half_band, slot_count)
    updated = jnp.where(
        selector == 0, square, 2.0 * masked.astype(jnp.float32) - square
    ) * occupied.astype(jnp.float32)
    purity_part = jnp.sum(updated * updated)
    trace_part = jnp.sum(jnp.diagonal(updated[:, half_band], axis1=1, axis2=2))
    occupation, purity = (by_axis(trace_part, GRP_MEM), by_axis(purity_part, GRP_MEM))
    matrix_order = row_count * lax.axis_size(GRP) * lax.axis_size("mem") * tiles.shape[2]
    traces = jnp.stack([occupation, purity]) / matrix_order
    return (updated, traces)


def solution(mesh):
    torus = Mesh(
        mesh.devices.reshape(4, 4, 2, mesh.shape["mem"]), ("grp_0", "grp_1", "grp_2", "mem")
    )
    placed = (P(GRP_MEM, None, None, None), P(GRP_MEM, None), P(GRP_MEM))
    return jax.shard_map(
        on_device,
        mesh=torus,
        in_specs=placed,
        out_specs=(P(GRP_MEM, None, None, None), P()),
        check_vma=False,
    )
```

profile of v0, /device:TPU:0, one launch (start us, length us, event | category | flops | bytes accessed | tf_op | source)
XLA Modules:
  0.0 379.8 jit_solution(4653910757506806713)
XLA Ops:
  1.5 8.8 %constant_dynamic-update-slice_fusion.105 = (bf16[11,11,256,256]{3,2,0,1:T(8,128)(2,1)}, bf16[6,11,256,256]{3,2,0,1:T(8,128)(2,1)S(1)}) fusion(bf16[6,11]{0,1:T(8,128)(2,1)S(1)} %copy.98, bf16[6,11,256,256]{3,2,1,0:T(8,128)(2,1)} %param.27), kind=kLoop, calls=%fused_computation.196 | loop fusion | flops 17301504 | bytes 25952388
  17.3 5.2 %collective-permute-start = (bf16[5,5,256,256]{3,2,1,0:T(8,128)(2,1)}, bf16[5,5,256,256]{3,2,1,0:T(8,128)(2,1)}, u32[]{:S(2)}, u32[]{:S(2)}) collective-permute-start(bf16[5,5,256,256]{3,2,1,0:T(8,128)(2,1)} %get-tuple-element.192), channel_id=1, source_target_pairs={{0,1},{1,2},{2,3},{3,4},{4,5},{5,6},{6,7},{7,8},{8,9},{9,10},{10,1... | collective-permute-start | bytes 9830408 | tf_op jit(solution)/shard_map/ppermute | solution.py:14
  58.1 33.1 %collective-permute-done = bf16[5,5,256,256]{3,2,1,0:T(8,128)(2,1)} collective-permute-done((bf16[5,5,256,256]{3,2,1,0:T(8,128)(2,1)}, bf16[5,5,256,256]{3,2,1,0:T(8,128)(2,1)}, u32[]{:S(2)}, u32[]{:S(2)}) %collective-permute-start) | collective-permute-done | bytes 3276832 | tf_op jit(solution)/shard_map/ppermute | solution.py:14
  97.0 2.0 constant_dynamic-update-slice_fusion.40
  106.9 3.7 constant_dynamic-update-slice_fusion.52
  113.2 7.3 %constant_dynamic-update-slice_fusion.94 = (bf16[10,11,256,256]{3,2,0,1:T(8,128)(2,1)}, bf16[10,11,256,256]{3,2,0,1:T(8,128)(2,1)}, bf16[11,11,256,256]{3,2,0,1:T(8,128)(2,1)S(1)}) fusion(bf16[6,11,256,256]{3,2,0,1:T(8,128)(2,1)S(1)} %bitcast.565, bf16[10,11,256,256]{3,2,0,1:T(8,128)(2,1)} %get-tuple-element.259, ...), kind=kLoop, calls=%fused_computation.185 | loop fusion | bytes 34603008
  120.6 4.9 %fusion.28 = f32[6,6,256,256]{3,2,0,1:T(8,128)} fusion(bf16[11,11,256,256]{3,2,0,1:T(8,128)(2,1)S(1)} %get-tuple-element.190, bf16[6,11,256,256]{3,2,0,1:T(8,128)(2,1)S(1)} %bitcast.565), kind=kOutput, calls=%fused_computation.48 | convolution fusion | flops 1207959552 | bytes 14942208 | tf_op jit(solution)/shard_map/rab,rqbc->rqac/dot_general | solution.py:30
  125.5 12.0 %scatter-add.34 = f32[6,11,256,256]{3,2,0,1:T(8,128)} pad(f32[6,6,256,256]{3,2,0,1:T(8,128)} %fusion.28, f32[]{:T(128)} %constant.303.clone.1), padding=0_0x0_5x0_0x0_0 | pad | bytes 26738692 | tf_op jit(solution)/shard_map/scatter-add | solution.py:35
  137.5 12.0 %fusion.4 = f32[6,11,256,256]{3,2,0,1:T(8,128)} fusion(f32[6,11,256,256]{3,2,0,1:T(8,128)} %scatter-add.34, bf16[10,11,256,256]{3,2,0,1:T(8,128)(2,1)} %get-tuple-element.189, bf16[6,11,256,256]{3,2,0,1:T(8,128)(2,1)} %copy-done), kind=kOutput, calls=%fused_computation.16 | convolution fusion | flops 1412038656 | bytes 28311552 | tf_op jit(solution)/shard_map/rab,rqbc->rqac/dot_general | solution.py:30
  149.5 10.6 %fusion.3 = f32[6,11,256,256]{3,2,0,1:T(8,128)} fusion(f32[6,11,256,256]{3,2,0,1:T(8,128)} %fusion.4, bf16[6,11,256,256]{3,2,0,1:T(8,128)(2,1)} %copy-done, bf16[1,11,256,256]{3,2,0,1:T(8,128)(2,1)S(1)} %bitcast.574, bf16[1,11,256,256]{3,2,0,1:T(8,128)(2,1)S(1)} %bitcast.577, bf16[1,11,256,256]{3,2,0,1:T(8,128)(2,1)} %bitcast.38), kind=kOutput, calls=%fused_computation.13 | convolution fusion | flops 1638924288 | bytes 38928384 | tf_op jit(solution)/shard_map/rab,rqbc->rqac/dot_general | solution.py:30
  160.2 11.9 %fusion.2 = f32[6,11,256,256]{3,2,0,1:T(8,128)} fusion(f32[6,11,256,256]{3,2,0,1:T(8,128)} %fusion.3, bf16[6,11,256,256]{3,2,0,1:T(8,128)(2,1)} %copy-done, bf16[1,11,256,256]{3,2,0,1:T(8,128)(2,1)S(1)} %bitcast.575, bf16[1,11,256,256]{3,2,0,1:T(8,128)(2,1)S(1)} %bitcast.578), kind=kOutput, calls=%fused_computation.10 | convolution fusion | flops 1836711936 | bytes 40632320 | tf_op jit(solution)/shard_map/rab,rqbc->rqac/dot_general | solution.py:30
  172.1 14.4 %fusion.1 = f32[6,11,256,256]{3,2,0,1:T(8,128)} fusion(f32[6,11,256,256]{3,2,0,1:T(8,128)} %fusion.2, bf16[6,11,256,256]{3,2,0,1:T(8,128)(2,1)} %copy-done, bf16[1,11,256,256]{3,2,0,1:T(8,128)(2,1)S(1)} %bitcast.576), kind=kOutput, calls=%fused_computation.7 | convolution fusion | flops 2032926720 | bytes 42336256 | tf_op jit(solution)/shard_map/rab,rqbc->rqac/dot_general | solution.py:30
  186.5 17.4 %bitcast_add_fusion = f32[6,11,256,256]{3,2,0,1:T(8,128)} fusion(f32[6,11,256,256]{3,2,0,1:T(8,128)} %fusion.1, bf16[6,11,256,256]{3,2,0,1:T(8,128)(2,1)} %copy-done), kind=kOutput, calls=%fused_computation.3 | convolution fusion | flops 2218917888 | bytes 44040192 | tf_op jit(solution)/shard_map/rab,rqbc->rqac/dot_general | solution.py:30
  209.7 1.9 constant_dynamic-update-slice_fusion.97
  211.6 1.9 constant_dynamic-update-slice_fusion.96
  217.6 16.8 %constant_dynamic-update-slice_fusion.109 = (f32[6,11,256,256]{3,2,0,1:T(8,128)}, f32[6,10,256,256]{3,2,0,1:T(8,128)}) fusion(f32[6,11,256,256]{3,2,0,1:T(8,128)} %bitcast_add_fusion, bf16[1,11,256,256]{3,2,0,1:T(8,128)(2,1)S(1)} %bitcast.568, bf16[6,11,256,256]{3,2,0,1:T(8,128)(2,1)} %copy-done), kind=kOutput, calls=%fused_computation.250 | convolution fusion | flops 2032926720 | bytes 58064896 | tf_op jit(solution)/shard_map/rab,rqbc->rqac/dot_general | solution.py:30
  234.4 1.9 constant_dynamic-update-slice_fusion.104
  238.2 3.3 constant_dynamic-update-slice_fusion.102
  241.5 3.2 bitcast_dynamic-update-slice_fusion
  244.7 2.6 bitcast_dynamic-update-slice_fusion.5
  247.3 14.7 %constant_dynamic-update-slice_fusion.108 = (f32[6,11,256,256]{3,2,0,1:T(8,128)}, f32[6,9,256,256]{3,2,0,1:T(8,128)}) fusion(f32[6,11,256,256]{3,2,0,1:T(8,128)} %get-tuple-element.269, bf16[1,11,256,256]{3,2,0,1:T(8,128)(2,1)S(1)} %bitcast.572, bf16[1,11,256,256]{3,2,0,1:T(8,128)(2,1)S(1)} %bitcast.569, bf16[6,11,256,256]{3,2,0,1:T(8,128)(2,1)} %copy-done, ...), kind=kOutput, calls=%fused_computation.249 | convolution fusion | flops 1836711936 | bytes 54788096 | tf_op jit(solution)/shard_map/rab,rqbc->rqac/dot_general | solution.py:30
  262.0 15.2 %constant_dynamic-update-slice_fusion.107 = (f32[6,11,256,256]{3,2,0,1:T(8,128)}, f32[6,8,256,256]{3,2,0,1:T(8,128)}) fusion(f32[6,11,256,256]{3,2,0,1:T(8,128)} %get-tuple-element.271, bf16[1,11,256,256]{3,2,0,1:T(8,128)(2,1)} %bitcast.172, bf16[1,11,256,256]{3,2,0,1:T(8,128)(2,1)} %bitcast.573, bf16[1,11,256,256]{3,2,0,1:T(8,128)(2,1)} %bitcast.570, ...), kind=kOutput, calls=%fused_computation.248 | convolution fusion | flops 1638924288 | bytes 51511296 | tf_op jit(solution)/shard_map/rab,rqbc->rqac/dot_general | solution.py:30
  277.2 15.6 %constant_dynamic-update-slice_fusion.106 = (f32[6,11,256,256]{3,2,0,1:T(8,128)}, f32[6,7,256,256]{3,2,0,1:T(8,128)}) fusion(f32[6,11,256,256]{3,2,0,1:T(8,128)} %get-tuple-element.273, bf16[10,11,256,256]{3,2,0,1:T(8,128)(2,1)} %get-tuple-element.252, bf16[6,11,256,256]{3,2,0,1:T(8,128)(2,1)} %copy-done, f32[6,8,256,256]{3,2,0,1:T(8,128)} %get-tuple-element.274), kind=kOutput, calls=%fused_computation.247 | convolution fusion | flops 1412038656 | bytes 39321600 | tf_op jit(solution)/shard_map/rab,rqbc->rqac/dot_general | solution.py:30
  292.8 10.3 %fusion.5 = f32[6,11,256,256]{3,2,0,1:T(8,128)} fusion(f32[6,11,256,256]{3,2,0,1:T(8,128)} %get-tuple-element.275, f32[6,7,256,256]{3,2,0,1:T(8,128)} %get-tuple-element.276, bf16[11,11,256,256]{3,2,0,1:T(8,128)(2,1)} %bitcast_dynamic-update-slice_fusion.5, bf16[6,11,256,256]{3,2,0,1:T(8,128)(2,1)S(1)} %bitcast.567), kind=kOutput, calls=%fused_computation.18 | convolution fusion | flops 1210318848 | bytes 24379392 | tf_op jit(solution)/shard_map/rab,rqbc->rqac/dot_general | solution.py:30
  303.2 9.8 %multiply_reduce_fusion = (f32[]{:T(128)}, f32[6,11,256,256]{3,2,0,1:T(8,128)S(1)}) fusion(f32[6,11]{0,1:T(8,128)S(1)} %copy-done.27, f32[6,11,256,256]{3,2,0,1:T(8,128)} %fusion.5, bf16[6,11,256,256]{3,2,0,1:T(8,128)(2,1)S(1)} %bitcast.567, pred[6]{0:T(512)(128)(4,1)S(1)} %copy-done.28), kind=kLoop, calls=%fused_computation.4 | loop fusion | flops 30277632 | bytes 43254032 | tf_op jit(solution)/shard_map/reduce_sum | solution.py:92
  312.9 6.4 %copy.190 = f32[6,11,256,256]{3,2,1,0:T(8,128)} copy(f32[6,11,256,256]{3,2,0,1:T(8,128)S(1)} %get-tuple-element.155) | data formatting | bytes 34603008
  319.5 16.5 %copy.189 = f32[6,256,256]{0,2,1:T(8,128)} copy(f32[6,256,256]{2,1,0:T(8,128)S(1)} %slice_bitcast_fusion) | data formatting | bytes 3145728 | tf_op jit(solution)/shard_map/squeeze | solution.py:93
  336.0 2.3 gather_fusion
  338.9 17.5 %all-reduce.3 = (f32[]{:T(128)}, f32[]{:T(128)}) all-reduce(f32[]{:T(128)} %get-tuple-element.154, f32[]{:T(128)} %reduce_sum.18), channel_id=1, replica_groups=mesh['grp_0'=4,'grp_1'=4,'grp_2'=2,'mem'=4] {'grp_0'}, use_global_device_ids=true, to_apply=%region_6.0 | all-reduce | flops 2 | bytes 16 | tf_op jit(solution)/shard_map/psum | solution.py:19
  356.4 9.3 %all-reduce.2 = (f32[]{:T(128)}, f32[]{:T(128)}) all-reduce(f32[]{:T(128)} %get-tuple-element.150, f32[]{:T(128)} %get-tuple-element.151), channel_id=1, replica_groups=mesh['grp_0'=4,'grp_1'=4,'grp_2'=2,'mem'=4] {'grp_1'}, use_global_device_ids=true, to_apply=%region_7.0 | all-reduce | flops 2 | bytes 16 | tf_op jit(solution)/shard_map/psum | solution.py:19
  365.7 3.1 all-reduce.4
  368.8 9.1 %all-reduce.1 = (f32[1]{0:T(128)}, f32[1]{0:T(128)}) all-reduce(f32[1]{0:T(128)} %bitcast.212, f32[1]{0:T(128)} %bitcast.211), channel_id=1, replica_groups=mesh['grp_0'=4,'grp_1'=4,'grp_2'=2,'mem'=4] {'mem'}, use_global_device_ids=true, to_apply=%region_9.0 | all-reduce | flops 2 | bytes 16 | tf_op jit(solution)/shard_map/psum | solution.py:19
  (173 shorter events, 73.9 us)
Async XLA Ops:
  10.3 15.5 %copy-start = (bf16[6,11,256,256]{3,2,0,1:T(8,128)(2,1)}, bf16[6,11,256,256]{3,2,0,1:T(8,128)(2,1)S(1)}, u32[]{:S(2)}) copy-start(bf16[6,11,256,256]{3,2,0,1:T(8,128)(2,1)S(1)} %get-tuple-element.157) | copy-start | bytes 25952260
  17.3 74.0 %collective-permute-start = (bf16[5,5,256,256]{3,2,1,0:T(8,128)(2,1)}, bf16[5,5,256,256]{3,2,1,0:T(8,128)(2,1)}, u32[]{:S(2)}, u32[]{:S(2)}) collective-permute-start(bf16[5,5,256,256]{3,2,1,0:T(8,128)(2,1)} %get-tuple-element.192), channel_id=1, source_target_pairs={{0,1},{1,2},{2,3},{3,4},{4,5},{5,6},{6,7},{7,8},{8,9},{9,10},{10,1... | collective-permute-start | bytes 9830408 | tf_op jit(solution)/shard_map/ppermute | solution.py:14
  22.5 181.4 %collective-permute-start.1 = (bf16[5,5,256,256]{3,2,1,0:T(8,128)(2,1)}, bf16[5,5,256,256]{3,2,1,0:T(8,128)(2,1)}, u32[]{:S(2)}, u32[]{:S(2)}) collective-permute-start(bf16[5,5,256,256]{3,2,1,0:T(8,128)(2,1)} %get-tuple-element.191), channel_id=1, source_target_pairs={{1,0},{2,1},{3,2},{4,3},{5,4},{6,5},{7,6},{8,7},{9,8},{10,9},{11,1... | collective-permute-start | bytes 9830408 | tf_op jit(solution)/shard_map/ppermute | solution.py:14
  41.7 7.8 %copy-start.29 = (s32[6]{0:T(128)S(1)}, s32[6]{0:T(128)}, u32[]{:S(2)}) copy-start(s32[6]{0:T(128)} %param.29) | copy-start | bytes 76
  49.4 7.9 %copy-start.22 = (bf16[1,1,256,256]{2,3,1,0:T(8,128)(2,1)S(1)}, bf16[1,1,256,256]{2,3,1,0:T(8,128)(2,1)}, u32[]{:S(2)}) copy-start(bf16[1,1,256,256]{2,3,1,0:T(8,128)(2,1)} %copy.244) | copy-start | bytes 393220
  49.4 7.9 %copy-start.21 = (bf16[1,1,256,256]{2,3,1,0:T(8,128)(2,1)S(1)}, bf16[1,1,256,256]{2,3,1,0:T(8,128)(2,1)}, u32[]{:S(2)}) copy-start(bf16[1,1,256,256]{2,3,1,0:T(8,128)(2,1)} %copy.245) | copy-start | bytes 393220
  49.4 8.0 %copy-start.23 = (bf16[1,1,256,256]{2,3,1,0:T(8,128)(2,1)S(1)}, bf16[1,1,256,256]{2,3,1,0:T(8,128)(2,1)}, u32[]{:S(2)}) copy-start(bf16[1,1,256,256]{2,3,1,0:T(8,128)(2,1)} %copy.249) | copy-start | bytes 393220
  49.4 8.0 %copy-start.24 = (bf16[1,1,256,256]{2,3,1,0:T(8,128)(2,1)S(1)}, bf16[1,1,256,256]{2,3,1,0:T(8,128)(2,1)}, u32[]{:S(2)}) copy-start(bf16[1,1,256,256]{2,3,1,0:T(8,128)(2,1)} %copy.251) | copy-start | bytes 393220
  50.6 7.5 %copy-start.25 = (bf16[1,1,256,256]{2,3,1,0:T(8,128)(2,1)S(1)}, bf16[1,1,256,256]{2,3,1,0:T(8,128)(2,1)}, u32[]{:S(2)}) copy-start(bf16[1,1,256,256]{2,3,1,0:T(8,128)(2,1)} %copy.237) | copy-start | bytes 393220
  50.6 7.5 %copy-start.26 = (bf16[1,1,256,256]{2,3,1,0:T(8,128)(2,1)S(1)}, bf16[1,1,256,256]{2,3,1,0:T(8,128)(2,1)}, u32[]{:S(2)}) copy-start(bf16[1,1,256,256]{2,3,1,0:T(8,128)(2,1)} %copy.246) | copy-start | bytes 393220
  51.9 39.3 %copy-start.4 = (bf16[11,256,256]{2,1,0:T(8,128)(2,1)S(1)}, bf16[11,256,256]{2,1,0:T(8,128)(2,1)}, u32[]{:S(2)}) copy-start(bf16[11,256,256]{2,1,0:T(8,128)(2,1)} %constant_dynamic-update-slice_fusion.44) | copy-start | bytes 4325380
  51.9 39.3 %copy-start.7 = (bf16[11,256,256]{2,1,0:T(8,128)(2,1)S(1)}, bf16[11,256,256]{2,1,0:T(8,128)(2,1)}, u32[]{:S(2)}) copy-start(bf16[11,256,256]{2,1,0:T(8,128)(2,1)} %get-tuple-element.277) | copy-start | bytes 4325380
  97.0 3.9 %copy-start.20 = (bf16[1,1,256,256]{2,3,1,0:T(8,128)(2,1)S(1)}, bf16[1,1,256,256]{2,3,1,0:T(8,128)(2,1)}, u32[]{:S(2)}) copy-start(bf16[1,1,256,256]{2,3,1,0:T(8,128)(2,1)} %copy.218) | copy-start | bytes 393220
  101.6 11.7 %slice-start = ((s8[8650752]{0:T(1024)(128)(4,1)}), s8[4194304]{0:T(1024)(128)(4,1)S(1)}, s32[]{:S(2)}) async-start(s8[8650752]{0:T(1024)(128)(4,1)} %bitcast.564), calls=%async_computation | async-start | bytes 8388608
  103.3 2.7 copy-start.15
  103.3 3.4 copy-start.8
  103.3 3.4 copy-start.14
  103.3 3.4 copy-start.13
  103.3 3.4 copy-start.12
  104.7 8.6 %slice-start.1 = ((s8[8650752]{0:T(1024)(128)(4,1)}), s8[4194304]{0:T(1024)(128)(4,1)S(1)}, s32[]{:S(2)}) async-start(s8[8650752]{0:T(1024)(128)(4,1)} %bitcast.564), calls=%async_computation.1 | async-start | bytes 8388608
  106.8 3.8 copy-start.9
  106.9 5.0 %copy-start.5 = (bf16[11,256,256]{2,1,0:T(8,128)(2,1)}, bf16[11,256,256]{2,1,0:T(8,128)(2,1)S(1)}, u32[]{:S(2)}) copy-start(bf16[11,256,256]{2,1,0:T(8,128)(2,1)S(1)} %constant_dynamic-update-slice_fusion.34) | copy-start | bytes 4325380
  137.5 12.0 %copy-start.6 = (bf16[11,256,256]{2,1,0:T(8,128)(2,1)S(1)}, bf16[11,256,256]{2,1,0:T(8,128)(2,1)}, u32[]{:S(2)}) copy-start(bf16[11,256,256]{2,1,0:T(8,128)(2,1)} %copy-done.5) | copy-start | bytes 4325380
  137.5 12.0 %copy-start.10 = (bf16[11,256,256]{2,1,0:T(8,128)(2,1)S(1)}, bf16[11,256,256]{2,1,0:T(8,128)(2,1)}, u32[]{:S(2)}) copy-start(bf16[11,256,256]{2,1,0:T(8,128)(2,1)} %copy-done.9) | copy-start | bytes 4325380
  213.5 33.7 %copy-start.1 = (bf16[11,256,256]{2,1,0:T(8,128)(2,1)}, bf16[11,256,256]{2,1,0:T(8,128)(2,1)S(1)}, u32[]{:S(2)}) copy-start(bf16[11,256,256]{2,1,0:T(8,128)(2,1)S(1)} %constant_dynamic-update-slice_fusion.53) | copy-start | bytes 4325380
  213.6 33.7 %copy-start.3 = (bf16[11,256,256]{2,1,0:T(8,128)(2,1)}, bf16[11,256,256]{2,1,0:T(8,128)(2,1)S(1)}, u32[]{:S(2)}) copy-start(bf16[11,256,256]{2,1,0:T(8,128)(2,1)S(1)} %constant_dynamic-update-slice_fusion.64) | copy-start | bytes 4325380
  262.0 30.8 %slice-start.3 = ((s8[8650752]{0:T(1024)(128)(4,1)}), s8[4194304]{0:T(1024)(128)(4,1)S(1)}, s32[]{:S(2)}) async-start(s8[8650752]{0:T(1024)(128)(4,1)} %bitcast.566), calls=%async_computation.3 | async-start | bytes 8388608
  262.0 30.8 %slice-start.4 = ((s8[8650752]{0:T(1024)(128)(4,1)}), s8[262144]{0:T(1024)(128)(4,1)S(1)}, s32[]{:S(2)}) async-start(s8[8650752]{0:T(1024)(128)(4,1)} %bitcast.566), calls=%async_computation.4 | async-start | bytes 524288
  277.2 15.6 %slice-start.5 = ((s8[8650752]{0:T(1024)(128)(4,1)}), s8[4194304]{0:T(1024)(128)(4,1)S(1)}, s32[]{:S(2)}) async-start(s8[8650752]{0:T(1024)(128)(4,1)} %bitcast.566), calls=%async_computation.5 | async-start | bytes 8388608
  292.8 10.4 %copy-start.27 = (f32[6,11]{0,1:T(8,128)S(1)}, f32[6,11]{0,1:T(8,128)}, u32[]{:S(2)}) copy-start(f32[6,11]{0,1:T(8,128)} %copy.188) | copy-start | bytes 796
  292.8 10.4 %copy-start.28 = (pred[6]{0:T(512)(128)(4,1)S(1)}, pred[6]{0:T(512)(128)(4,1)}, u32[]{:S(2)}) copy-start(pred[6]{0:T(512)(128)(4,1)} %broadcast_compare_fusion) | copy-start | bytes 22
  319.5 16.5 %copy-start.2 = (s32[256,1]{0,1:T(1,128)S(1)}, s32[256,1]{0,1:T(1,128)}, u32[]{:S(2)}) copy-start(s32[256,1]{0,1:T(1,128)} %shift-left_or_fusion) | copy-start | bytes 3076
  (6 other events, 12.9 us)
where the time goes:
time: 381 us; the launch traced here: 380 us
  matrix products  144 us (38%)
  local copies, waits for them, and re-layouts  133 us (35%)
  blocking collectives  39 us (10%)
  waiting for transfers between devices  33.1 us (9%)
  other arithmetic  22.9 us (6%)
  starting transfers between devices  6.46 us (2%)
    dot_general x11, matrix products, band_square(): jnp.einsum('rab,rqbc->rqac', left_tile, right_tiles, preferred_element_ty...  144 us
    unnamed x157, local copies, waits for them, and re-layouts  92.8 us
    psum x4, blocking collectives, by_axis(): array = lax.psum(array, axis)  39 us
    ppermute x2, waiting for transfers between devices, from_behind(): lax.ppermute(value, axis, [(source, source + steps) for source in range(f...  33.1 us
    squeeze x2, local copies, waits for them, and re-layouts, on_device(): trace_part = jnp.sum(jnp.diagonal(updated[:, half_band], axis1=1, axis2=2))  16.6 us
    scatter-add x1, local copies, waits for them, and re-layouts, band_square(): total = total.at[:, low_out:high_out].add(product)  12 us
    reduce_sum x1, other arithmetic, on_device(): purity_part = jnp.sum(updated * updated)  9.76 us
    unnamed x3, other arithmetic  8.84 us
  transfers between devices with their start and end apart: 2, of which 1 were waited for; matrix products, arithmetic and copies ran while one was open for 39% of the time, Pallas kernels for 0%

commit v1 on v0

v1 whole, which is shorter than its diff:
```python
import jax
import jax.numpy as jnp
from jax import lax
from jax.experimental import pallas as pl
from jax.experimental.pallas import tpu as pltpu
from jax.sharding import Mesh
from jax.sharding import PartitionSpec as P

GRP_MEM = ("grp_0", "grp_1", "grp_2", "mem")
GRP = ("grp_0", "grp_1", "grp_2")
TILE = 256
HALF = 128
ROWS = 6
BAND = 5
SLOTS = 11
EXTRA = 16
MIB = 2**20

NEAR = ((1, 5), (2, 5), (3, 4), (3, 5), (4, 5), (3, 3), (4, 4), (5, 5))
FAR = ((1, 2), (1, 3), (1, 4), (2, 3), (2, 4), (1, 1), (2, 2))


def full_of(pairs):
    return [pair for pair in pairs if pair[0] != pair[1]]


def diag_of(pairs):
    return [pair for pair in pairs if pair[0] == pair[1]]


def chunk_rows(pairs):
    return TILE * len(full_of(pairs)) + HALF * len(diag_of(pairs)) + EXTRA


def shift(value, steps):
    count = lax.axis_size(GRP_MEM)
    first, last = max(0, -steps), min(count, count - steps)
    return lax.ppermute(value, GRP_MEM, [(source, source + steps) for source in range(first, last)])


def iotas(shape):
    return lax.broadcasted_iota(jnp.int32, shape, 0), lax.broadcasted_iota(jnp.int32, shape, 1)


def smem():
    return pl.BlockSpec(memory_space=pltpu.SMEM)


def vmem():
    return pl.BlockSpec(memory_space=pltpu.VMEM)


def hbm():
    return pl.BlockSpec(memory_space=pltpu.HBM)


def params(mib):
    return pltpu.CompilerParams(vmem_limit_bytes=mib * MIB)


def cost(products, tiles_moved):
    return pl.CostEstimate(
        flops=2 * TILE**3 * products, bytes_accessed=tiles_moved * TILE * TILE * 2, transcendentals=0
    )


def pack_corners(tiles, mask, branch, plan, name):
    diag_count = sum(len(diag_of(pairs)) for pairs, _ in plan)
    copy_count = sum(len(pairs) for pairs, _ in plan)

    def body(mask_ref, branch_ref, tiles_ref, *refs):
        outs, (diag_ref, sems) = refs[: len(plan)], refs[len(plan) :]
        copies = []
        diag = 0
        for (pairs, first_row), out in zip(plan, outs):
            for place, (p, q) in enumerate(full_of(pairs)):
                row, slot = p - 1 + first_row, q - p + BAND
                target = out.at[pl.ds(place * TILE, TILE)]
                copies.append((tiles_ref.at[row, slot], target))
            for p, _ in diag_of(pairs):
                copies.append((tiles_ref.at[p - 1 + first_row, BAND], diag_ref.at[diag]))
                diag += 1
        copies = [
            pltpu.make_async_copy(source, target, sems.at[number])
            for number, (source, target) in enumerate(copies)
        ]
        for copy in copies:
            copy.start()
        rows, columns = iotas((HALF, HALF))
        extra_rows, _ = iotas((EXTRA, TILE))
        number = 0
        diag = 0
        for (pairs, first_row), out in zip(plan, outs):
            for place, (p, q) in enumerate(full_of(pairs)):
                row, slot = p - 1 + first_row, q - p + BAND
                copies[number].wait()
                number += 1

                @pl.when(mask_ref[row, slot] == 0)
                def _(out=out, place=place):
                    out[pl.ds(place * TILE, TILE), :] = jnp.zeros((TILE, TILE), jnp.bfloat16)

            base = TILE * len(full_of(pairs))
            extra = jnp.zeros((EXTRA, TILE), jnp.float32)
            for place, (p, _) in enumerate(diag_of(pairs)):
                copies[number].wait()
                number += 1
                keep = mask_ref[p - 1 + first_row, BAND].astype(jnp.float32)
                tile = diag_ref[diag].astype(jnp.float32) * keep
                diag += 1
                low = tile[HALF:, HALF:]
                folded = jnp.where(columns <= rows, tile[:HALF, :HALF], low)
                at = pl.ds(base + place * HALF, HALF)
                out[at, pl.ds(0, HALF)] = tile[HALF:, :HALF].astype(jnp.bfloat16)
                out[at, pl.ds(HALF, HALF)] = folded.astype(jnp.bfloat16)
                line = jnp.sum(jnp.where(columns == rows, low, 0.0), axis=0, keepdims=True)
                line = jnp.concatenate([line, line], axis=1)
                extra = jnp.where(extra_rows == place, line, extra)
            for p in range(1, BAND + 1):
                flag = jnp.where(branch_ref[p - 1 + first_row] == 0, 0.0, 1.0)
                extra = jnp.where(extra_rows == 7 + p, flag, extra)
            out[pl.ds(base + HALF * len(diag_of(pairs)), EXTRA), :] = extra.astype(jnp.bfloat16)

    return pl.pallas_call(
        body,
        out_shape=[
            jax.ShapeDtypeStruct((chunk_rows(pairs), TILE), jnp.bfloat16) for pairs, _ in plan
        ],
        in_specs=[smem(), smem(), hbm()],
        out_specs=[vmem() for _ in plan],
        scratch_shapes=[
            pltpu.VMEM((diag_count, TILE, TILE), jnp.bfloat16),
            pltpu.SemaphoreType.DMA((copy_count,)),
        ],
        compiler_params=params(16),
        cost_estimate=cost(1, 4 * copy_count),
        name=name,
    )(mask, branch, tiles)


class Corner:
    def __init__(self, square_ref):
        self.square_ref = square_ref
        self.where = {}
        self.count = 0

    def add(self, chunk, pairs):
        rows, columns = iotas((HALF, HALF))
        for place, pair in enumerate(full_of(pairs)):
            self.where[pair] = (chunk, pl.ds(place * TILE, TILE))
        base = TILE * len(full_of(pairs))
        extra = chunk[pl.ds(base + HALF * len(diag_of(pairs)), EXTRA), :].astype(jnp.float32)
        for place, pair in enumerate(diag_of(pairs)):
            at = pl.ds(base + place * HALF, HALF)
            corner = chunk[at, pl.ds(0, HALF)].astype(jnp.float32)
            folded = chunk[at, pl.ds(HALF, HALF)].astype(jnp.float32)
            turned = folded.T
            line = extra[place : place + 1, :HALF]
            high = jnp.where(columns <= rows, folded, turned)
            low = jnp.where(columns > rows, folded, turned)
            low = jnp.where(columns == rows, line, low)
            target = self.square_ref.at[self.count]
            target[pl.ds(0, HALF), pl.ds(0, HALF)] = high.astype(jnp.bfloat16)
            target[pl.ds(HALF, HALF), pl.ds(HALF, HALF)] = low.astype(jnp.bfloat16)
            target[pl.ds(HALF, HALF), pl.ds(0, HALF)] = corner.astype(jnp.bfloat16)
            target[pl.ds(0, HALF), pl.ds(HALF, HALF)] = corner.T.astype(jnp.bfloat16)
            self.where[pair] = (target, slice(None))
            self.count += 1
        return extra

    def times(self, left, p, q):
        chunk, at = self.where[(min(p, q), max(p, q))]
        return dot(left, chunk[at, :], p > q)


def dot(left, right, transposed):
    return lax.dot_general(
        left, right, (((1,), (1 if transposed else 0,)), ((), ())), preferred_element_type=jnp.float32
    )


def polynomial(square, own, keep, bent):
    return (keep * (1.0 - 2.0 * bent)) * square + (keep * (2.0 * bent)) * own


def squares(value):
    return jnp.sum((value * value).reshape(TILE // 8, 8, TILE), axis=0)


def scalars(mask_ref, branch_ref, row, slot):
    keep = mask_ref[row, slot].astype(jnp.float32)
    bent = jnp.where(branch_ref[row] == 0, 0.0, 1.0)
    return keep, bent


def inner_tiles(tiles, mask, branch, after):
    inner = [(i, j) for i in range(ROWS) for j in range(ROWS)]

    def body(mask_ref, branch_ref, tiles_ref, _, out_ref, sums_ref, own_ref, new_ref, in_sems, out_sems):
        loads = [
            pltpu.make_async_copy(tiles_ref.at[row], own_ref.at[row], in_sems.at[row])
            for row in range(ROWS)
        ]
        for load in loads:
            load.start()
        for row, load in enumerate(loads):
            load.wait()
            for slot in range(SLOTS):

                @pl.when(mask_ref[row, slot] == 0)
                def _(row=row, slot=slot):
                    own_ref[row, slot] = jnp.zeros((TILE, TILE), jnp.bfloat16)

        rows, columns = iotas((TILE, TILE))
        total = jnp.zeros((8, TILE), jnp.float32)
        trace = jnp.zeros((8, TILE), jnp.float32)
        stores = []

        def emit(i, j, square):
            slot = j - i + BAND
            keep, bent = scalars(mask_ref, branch_ref, i, slot)
            value = polynomial(square, own_ref[i, slot].astype(jnp.float32), keep, bent)
            number = i * ROWS + j
            new_ref[number] = value
            stores.append(
                pltpu.make_async_copy(new_ref.at[number], out_ref.at[i, slot], out_sems.at[number])
            )
            stores[-1].start()
            return value

        for i in range(ROWS):
            for j in range(i, ROWS):
                square = None
                for k in range(j - BAND, i + BAND + 1):
                    left = own_ref[i, k - i + BAND]
                    if 0 <= k < ROWS:
                        term = dot(left, own_ref[k, j - k + BAND], False)
                    else:
                        term = dot(left, own_ref[j, k - j + BAND], True)
                    square = term if square is None else square + term
                value = emit(i, j, square)
                total = total + squares(value)
                if i == j:
                    part = jnp.where(rows == columns, value, 0.0)
                    trace = trace + jnp.sum(part.reshape(TILE // 8, 8, TILE), axis=0)
                else:
                    total = total + squares(emit(j, i, square.T))
        sums_ref[pl.ds(0, 8), :] = total
        sums_ref[pl.ds(8, 8), :] = trace
        for store in stores:
            store.wait()

    return pl.pallas_call(
        body,
        out_shape=[
            jax.ShapeDtypeStruct((ROWS, SLOTS, TILE, TILE), jnp.float32),
            jax.ShapeDtypeStruct((16, TILE), jnp.float32),
        ],
        in_specs=[smem(), smem(), hbm(), hbm()],
        out_specs=[hbm(), vmem()],
        scratch_shapes=[
            pltpu.VMEM((ROWS, SLOTS, TILE, TILE), jnp.bfloat16),
            pltpu.VMEM((len(inner), TILE, TILE), jnp.float32),
            pltpu.SemaphoreType.DMA((ROWS,)),
            pltpu.SemaphoreType.DMA((len(inner),)),
        ],
        compiler_params=params(32),
        cost_estimate=cost(196, 66 + 72),
        name="inner",
    )(mask, branch, tiles, after)


def cross_tiles(tiles, mask, branch, made, above, below, up_pairs, down_pairs, sums, name):
    outputs = []
    for r, q in up_pairs:
        i, j = r - 1, q - 6
        terms = [((i, k - i + BAND), ("own", k, j - k + BAND)) for k in range(q)]
        terms += [((i, p - 6 - i + BAND), ("above", p, q)) for p in range(r, BAND + 1)]
        outputs.append((i, j - i + BAND, terms, ("above", q)))
    for r, q in down_pairs:
        i, j = q, 5 + r
        terms = [((i, k - i + BAND), ("own", k, j - k + BAND)) for k in range(r, ROWS)]
        terms += [((i, 5 + p - i + BAND), ("below", p, r)) for p in range(1, q + 1)]
        outputs.append((i, j - i + BAND, terms, ("below", r)))
    needed = []
    for i, slot, terms, _ in outputs:
        for left, right in terms:
            needed += [left] + ([right[1:]] if right[0] == "own" else [])
        needed.append((i, slot))
    needed = list(dict.fromkeys(needed))
    place = {key: number for number, key in enumerate(needed)}
    chunks = [("above", pairs, chunk) for pairs, chunk in above]
    chunks += [("below", pairs, chunk) for pairs, chunk in below]
    diag_count = {
        side: sum(len(diag_of(pairs)) for which, pairs, _ in chunks if which == side)
        for side in ("above", "below")
    }
    reduce = sums is not None
    group = 1
    if reduce:
        for axis in GRP:
            group *= lax.axis_size(axis)

    def body(mask_ref, branch_ref, tiles_ref, _, *refs):
        refs = list(refs)
        landed = [refs.pop(0) for _ in chunks]
        sums_ref = refs.pop(0) if reduce else None
        out_ref = refs.pop(0)
        red_ref = refs.pop(0) if reduce else None
        own_ref, above_ref, below_ref, new_ref, in_sems, out_sems = refs
        loads = [
            pltpu.make_async_copy(tiles_ref.at[row, slot], own_ref.at[number], in_sems.at[number])
            for number, (row, slot) in enumerate(needed)
        ]
        for load in loads:
            load.start()
        corners = {"above": Corner(above_ref), "below": Corner(below_ref)}
        flags = {}
        for (side, pairs, _), chunk_ref in zip(chunks, landed):
            flags.setdefault(side, corners[side].add(chunk_ref, pairs))
        ready = set()

        def own(row, slot):
            number = place[(row, slot)]
            if number not in ready:
                ready.add(number)
                loads[number].wait()
                keep = mask_ref[row, slot].astype(jnp.float32).astype(jnp.bfloat16)
                own_ref[number] = own_ref[number] * keep
            return own_ref[number]

        total = jnp.zeros((8, TILE), jnp.float32)
        stores = []
        for number, (i, slot, terms, (side, other)) in enumerate(outputs):
            square = None
            for left, right in terms:
                if right[0] == "own":
                    term = dot(own(*left), own(*right[1:]), False)
                else:
                    term = corners[right[0]].times(own(*left), *right[1:])
                square = term if square is None else square + term
            keep, bent = scalars(mask_ref, branch_ref, i, slot)
            mine = own(i, slot).astype(jnp.float32)
            value = polynomial(square, mine, keep, bent)
            new_ref[number] = value
            stores.append(
                pltpu.make_async_copy(new_ref.at[number], out_ref.at[i, slot], out_sems.at[number])
            )
            stores[-1].start()
            if reduce:
                bent = flags[side][7 + other : 8 + other, :]
                mirror = polynomial(square, mine, keep, bent)
                total = total + squares(value) + squares(mirror)
        if reduce:
            purity = jnp.sum(total + sums_ref[pl.ds(0, 8), :], keepdims=True)
            trace = jnp.sum(sums_ref[pl.ds(8, 8), :], keepdims=True)
            _, lanes = iotas((group, HALF))
            red_ref[...] = jnp.where(lanes == 0, trace, jnp.where(lanes == 1, purity, 0.0))
        for store in stores:
            store.wait()

    products = sum(len(terms) for _, _, terms, _ in outputs)
    out_shape = [jax.ShapeDtypeStruct(made.shape, made.dtype)]
    out_specs = [hbm()]
    if reduce:
        out_shape.append(jax.ShapeDtypeStruct((group, HALF), jnp.float32))
        out_specs.append(vmem())
    return pl.pallas_call(
        body,
        out_shape=out_shape,
        in_specs=[smem(), smem(), hbm(), hbm()] + [vmem() for _ in chunks] + [vmem()] * reduce,
        out_specs=out_specs,
        scratch_shapes=[
            pltpu.VMEM((len(needed), TILE, TILE), jnp.bfloat16),
            pltpu.VMEM((diag_count["above"], TILE, TILE), jnp.bfloat16),
            pltpu.VMEM((diag_count["below"], TILE, TILE), jnp.bfloat16),
            pltpu.VMEM((len(outputs), TILE, TILE), jnp.float32),
            pltpu.SemaphoreType.DMA((len(needed),)),
            pltpu.SemaphoreType.DMA((len(outputs),)),
        ],
        input_output_aliases={3: 0},
        compiler_params=params(32),
        cost_estimate=cost(products, 66 + 2 * len(outputs)),
        name=name,
    )(mask, branch, tiles, made, *[chunk for _, _, chunk in chunks], *([sums] if reduce else []))


def on_device(tiles, mask, branch):
    tiles, mask, branch = (
        pltpu.with_memory_space_constraint(value, pltpu.HBM) for value in (tiles, mask, branch)
    )
    down_first, up_first = pack_corners(tiles, mask, branch, ((NEAR, 1), (FAR, 0)), "pack_first")
    above_first, below_first = shift(down_first, 1), shift(up_first, -1)
    down_last, up_last = pack_corners(tiles, mask, branch, ((FAR, 1), (NEAR, 0)), "pack_last")
    above_last, below_last = shift(down_last, 1), shift(up_last, -1)
    made, sums = inner_tiles(tiles, mask, branch, up_last)
    made, part = cross_tiles(
        tiles, mask, branch, made, [(NEAR, above_first)], [(FAR, below_first)], NEAR, FAR, sums, "cross_first"
    )
    parts = lax.all_to_all(part, GRP, 0, 0, tiled=True)
    part = jnp.sum(parts, axis=0, keepdims=True)

    def partner(bits):
        return lax.ppermute(part, "mem", [(m, m ^ bits) for m in range(lax.axis_size("mem"))])

    others = [partner(bits) for bits in (1, 2, 3)]
    part, made = lax.optimization_barrier((part, made))
    (made,) = cross_tiles(
        tiles,
        mask,
        branch,
        made,
        [(NEAR, above_first), (FAR, above_last)],
        [(FAR, below_first), (NEAR, below_last)],
        FAR,
        NEAR,
        None,
        "cross_last",
    )
    traces = (part + others[0]) + (others[1] + others[2])
    order = ROWS * lax.axis_size(GRP_MEM) * TILE
    return made, traces[0, :2] / order


def solution(mesh):
    torus = Mesh(
        mesh.devices.reshape(4, 4, 2, mesh.shape["mem"]), ("grp_0", "grp_1", "grp_2", "mem")
    )
    placed = (P(GRP_MEM, None, None, None), P(GRP_MEM, None), P(GRP_MEM))
    return jax.shard_map(
        on_device,
        mesh=torus,
        in_specs=placed,
        out_specs=(P(GRP_MEM, None, None, None), P()),
        check_vma=False,
    )
```

time: 381 us -> 82.3 us (0.22)
  matrix products: 144 us -> 0 us
  local copies, waits for them, and re-layouts: 133 us -> 0 us
  Pallas kernels: 0 us -> 43.8 us
  waiting for transfers between devices: 33.1 us -> 0.02 us
  other arithmetic: 22.9 us -> 0.57 us
  blocking collectives: 39 us -> 21.8 us
  starting transfers between devices: 6.46 us -> 14.9 us
    dot_general x11 -> x0, matrix products: 144 us -> none  [band_square(): jnp.einsum('rab,rqbc->rqac', left_tile, right_tiles, preferred_element_ty...]
    unnamed x157 -> x0, local copies, waits for them, and re-layouts: 92.8 us -> none
    pallas_call x0 -> x5, Pallas kernels: none -> 43.8 us  [the longest x2 24.9 us: cross_tiles(): pl.pallas_call(body, out_shape=out_shape, in_specs=[smem(), smem(), hbm()...]
    psum x4 -> x0, blocking collectives: 39 us -> none  [by_axis(): array = lax.psum(array, axis)]
    ppermute x2 -> x7, waiting for transfers between devices: 33.1 us -> 0.02 us  [the longest x4 0.01 us: shift(): lax.ppermute(value, GRP_MEM, [(source, source + steps) for source in rang...]
    all_to_all x0 -> x1, blocking collectives: none -> 21.8 us  [on_device(): parts = lax.all_to_all(part, GRP, 0, 0, tiled=True)]
    squeeze x2 -> x0, local copies, waits for them, and re-layouts: 16.6 us -> none  [on_device(): trace_part = jnp.sum(jnp.diagonal(updated[:, half_band], axis1=1, axis2=2))]
    scatter-add x1 -> x0, local copies, waits for them, and re-layouts: 12 us -> none  [band_square(): total = total.at[:, low_out:high_out].add(product)]
  transfers between devices with their start and end apart: 2 -> 7, of which waited for: 1 -> 0; matrix products, arithmetic and copies ran while one was open for 39% -> 0% of each run, Pallas kernels for 0% -> 50%
where the time goes in v1:
time: 82.3 us; the launch traced here: 81.9 us
  Pallas kernels  43.8 us (53%)
  blocking collectives  21.8 us (26%)
  starting transfers between devices  14.9 us (18%)
    pallas_call x2, Pallas kernels, cross_tiles(): pl.pallas_call(body, out_shape=out_shape, in_specs=[smem(), smem(), hbm()...  24.9 us
    all_to_all x1, blocking collectives, on_device(): parts = lax.all_to_all(part, GRP, 0, 0, tiled=True)  21.8 us
    pallas_call x1, Pallas kernels, inner_tiles(): pl.pallas_call(body, out_shape=[jax.ShapeDtypeStruct((ROWS, SLOTS, TILE,...  12.8 us
    ppermute x4, starting transfers between devices, shift(): lax.ppermute(value, GRP_MEM, [(source, source + steps) for source in rang...  10.7 us
    pallas_call x2, Pallas kernels, pack_corners(): pl.pallas_call(body, out_shape=[jax.ShapeDtypeStruct((chunk_rows(pairs),...  6.07 us
    ppermute x3, starting transfers between devices, partner(): lax.ppermute(part, 'mem', [(m, m ^ bits) for m in range(lax.axis_size('me...  4.16 us
  transfers between devices with their start and end apart: 7, of which 0 were waited for; matrix products, arithmetic and copies ran while one was open for 0% of the time, Pallas kernels for 50%

profile of v1, /device:TPU:0, one launch (start us, length us, event | category | flops | bytes accessed | tf_op | source)
XLA Modules:
  0.0 81.9 jit_solution(9432097468144863036)
XLA Ops:
  0.6 2.5 %pack_first.1 = (bf16[1680,256]{1,0:T(8,128)(2,1)S(1)}, bf16[1552,256]{1,0:T(8,128)(2,1)S(1)}) custom-call(s32[6,11]{1,0:T(8,128)} %mask_ref.9, s32[6]{0:T(128)} %branch_ref.9, bf16[6,11,256,256]{3,2,1,0:T(8,128)(2,1)} %tiles_ref.9), custom_call_target="tpu_custom_call" | custom-call | flops 33554432 | bytes 7864320 | tf_op jit(solution)/shard_map/pack_first/pallas_call | solution.py:124
  3.1 3.6 %collective-permute-start = (bf16[1680,256]{1,0:T(8,128)(2,1)S(1)}, bf16[1680,256]{1,0:T(8,128)(2,1)S(1)}, u32[]{:S(2)}, u32[]{:S(2)}) collective-permute-start(bf16[1680,256]{1,0:T(8,128)(2,1)S(1)} %get-tuple-element.14), channel_id=1, source_target_pairs={{0,1},{1,2},{2,3},{3,4},{4,5},{5,6},{6,7},{7,8},{8,9},{9,10},{10,1... | collective-permute-start | bytes 2580488 | tf_op jit(solution)/shard_map/ppermute | solution.py:38
  6.7 1.3 %collective-permute-start.1 = (bf16[1552,256]{1,0:T(8,128)(2,1)S(1)}, bf16[1552,256]{1,0:T(8,128)(2,1)S(1)}, u32[]{:S(2)}, u32[]{:S(2)}) collective-permute-start(bf16[1552,256]{1,0:T(8,128)(2,1)S(1)} %get-tuple-element.15), channel_id=1, source_target_pairs={{1,0},{2,1},{3,2},{4,3},{5,4},{6,5},{7,6},{8,7},{9,8},{10,9},{11,1... | collective-permute-start | bytes 2383880 | tf_op jit(solution)/shard_map/ppermute | solution.py:38
  8.0 3.6 %pack_last.1 = (bf16[1552,256]{1,0:T(8,128)(2,1)}, bf16[1680,256]{1,0:T(8,128)(2,1)}) custom-call(s32[6,11]{1,0:T(8,128)} %mask_ref.9, s32[6]{0:T(128)} %branch_ref.9, bf16[6,11,256,256]{3,2,1,0:T(8,128)(2,1)} %tiles_ref.9), custom_call_target="tpu_custom_call" | custom-call | flops 33554432 | bytes 7864320 | tf_op jit(solution)/shard_map/pack_last/pallas_call | solution.py:124
  11.6 4.6 %collective-permute-start.2 = (bf16[1552,256]{1,0:T(8,128)(2,1)}, bf16[1552,256]{1,0:T(8,128)(2,1)S(1)}, u32[]{:S(2)}, u32[]{:S(2)}) collective-permute-start(bf16[1552,256]{1,0:T(8,128)(2,1)} %get-tuple-element.20), channel_id=1, source_target_pairs={{0,1},{1,2},{2,3},{3,4},{4,5},{5,6},{6,7},{7,8},{8,9},{9,10},{10,1... | collective-permute-start | bytes 2383880 | tf_op jit(solution)/shard_map/ppermute | solution.py:38
  16.2 1.3 %collective-permute-start.3 = (bf16[1680,256]{1,0:T(8,128)(2,1)}, bf16[1680,256]{1,0:T(8,128)(2,1)S(1)}, u32[]{:S(2)}, u32[]{:S(2)}) collective-permute-start(bf16[1680,256]{1,0:T(8,128)(2,1)} %get-tuple-element.12._), channel_id=1, source_target_pairs={{1,0},{2,1},{3,2},{4,3},{5,4},{6,5},{7,6},{8,7},{9,8},{10,9},{11,1... | collective-permute-start | bytes 2580488 | tf_op jit(solution)/shard_map/ppermute | solution.py:38
  17.5 12.8 %inner.1 = (f32[6,11,256,256]{3,2,1,0:T(8,128)}, f32[16,256]{1,0:T(8,128)S(1)}) custom-call(s32[6,11]{1,0:T(8,128)} %mask_ref.9, s32[6]{0:T(128)} %branch_ref.9, bf16[6,11,256,256]{3,2,1,0:T(8,128)(2,1)} %tiles_ref.9, bf16[1680,256]{1,0:T(8,128)(2,1)} %get-tuple-element.12._), custom_call_target="tpu_custom_call" | custom-call | flops 6576668672 | bytes 18087936 | tf_op jit(solution)/shard_map/inner/pallas_call | solution.py:253
  30.3 0.0 collective-permute-done.1.refs_1_.refs_2_
  30.3 0.0 collective-permute-done.refs_0_
  30.3 12.7 %cross_first.1 = (f32[6,11,256,256]{3,2,1,0:T(8,128)}, f32[32,128]{1,0:T(8,128)S(1)}) custom-call(s32[6,11]{1,0:T(8,128)} %mask_ref.9, s32[6]{0:T(128)} %branch_ref.9, bf16[6,11,256,256]{3,2,1,0:T(8,128)(2,1)} %tiles_ref.9, f32[6,11,256,256]{3,2,1,0:T(8,128)} %get-tuple-element.13._, ...), custom_call_target="tpu_custom_call", output_to_operand_aliasing={{0}: (3, {})} | custom-call | flops 3690987520 | bytes 12582912 | tf_op jit(solution)/shard_map/cross_first/pallas_call | solution.py:368
  43.1 21.8 %all_to_all.9 = f32[32,1,128]{2,1,0:T(1,128)S(1)} all-to-all(f32[32,1,128]{2,1,0:T(1,128)S(1)} %bitcast.6), channel_id=1, replica_groups=mesh['grp_0'=4,'grp_1'=4,'grp_2'=2,'mem'=4] {'grp_0','grp_1','grp_2'}, dimensions={0} | all-to-all | bytes 32768 | tf_op jit(solution)/shard_map/all_to_all | solution.py:400
  64.9 0.1 reduce_sum.9
  65.0 0.1 collective-permute-start.6
  65.1 0.0 collective-permute-start.5
  65.1 4.0 %collective-permute-start.4 = (f32[1,128]{1,0:T(1,128)S(1)}, f32[1,128]{1,0:T(1,128)S(1)}, u32[]{:S(2)}, u32[]{:S(2)}) collective-permute-start(f32[1,128]{1,0:T(1,128)S(1)} %bitcast.9), channel_id=1, source_target_pairs={{0,1},{1,0},{2,3},{3,2},{4,5},{5,4},{6,7},{7,6},{8,9},{9,8},{10,11... | collective-permute-start | bytes 1544 | tf_op jit(solution)/shard_map/ppermute | solution.py:404
  69.1 0.0 collective-permute-done.2.refs_1_
  69.1 0.0 collective-permute-done.3.refs_3_
  69.1 12.2 %cross_last.1 = f32[6,11,256,256]{3,2,1,0:T(8,128)} custom-call(s32[6,11]{1,0:T(8,128)} %mask_ref.9, s32[6]{0:T(128)} %branch_ref.9, bf16[6,11,256,256]{3,2,1,0:T(8,128)(2,1)} %tiles_ref.9, f32[6,11,256,256]{3,2,1,0:T(8,128)} %get-tuple-element.19._, bf16[1680,256]{1,0:T(8,128)(2,1)S(1)} %collective-permute-done.refs_0_, ...), custom_call_target="tpu_custom_call", output_to_operand_aliasing={{}: (3, {})} | custom-call | flops 3690987520 | bytes 12582912 | tf_op jit(solution)/shard_map/cross_last/pallas_call | solution.py:368
  81.3 0.0 collective-permute-done.6
  81.3 0.0 collective-permute-done.5
  81.3 0.0 collective-permute-done.4
  81.4 0.5 multiply_bitcast_fusion
  (1 shorter events, 0.0 us)
Async XLA Ops:
  3.1 27.2 %collective-permute-start = (bf16[1680,256]{1,0:T(8,128)(2,1)S(1)}, bf16[1680,256]{1,0:T(8,128)(2,1)S(1)}, u32[]{:S(2)}, u32[]{:S(2)}) collective-permute-start(bf16[1680,256]{1,0:T(8,128)(2,1)S(1)} %get-tuple-element.14), channel_id=1, source_target_pairs={{0,1},{1,2},{2,3},{3,4},{4,5},{5,6},{6,7},{7,8},{8,9},{9,10},{10,1... | collective-permute-start | bytes 2580488 | tf_op jit(solution)/shard_map/ppermute | solution.py:38
  6.7 23.7 %collective-permute-start.1 = (bf16[1552,256]{1,0:T(8,128)(2,1)S(1)}, bf16[1552,256]{1,0:T(8,128)(2,1)S(1)}, u32[]{:S(2)}, u32[]{:S(2)}) collective-permute-start(bf16[1552,256]{1,0:T(8,128)(2,1)S(1)} %get-tuple-element.15), channel_id=1, source_target_pairs={{1,0},{2,1},{3,2},{4,3},{5,4},{6,5},{7,6},{8,7},{9,8},{10,9},{11,1... | collective-permute-start | bytes 2383880 | tf_op jit(solution)/shard_map/ppermute | solution.py:38
  11.6 57.5 %collective-permute-start.2 = (bf16[1552,256]{1,0:T(8,128)(2,1)}, bf16[1552,256]{1,0:T(8,128)(2,1)S(1)}, u32[]{:S(2)}, u32[]{:S(2)}) collective-permute-start(bf16[1552,256]{1,0:T(8,128)(2,1)} %get-tuple-element.20), channel_id=1, source_target_pairs={{0,1},{1,2},{2,3},{3,4},{4,5},{5,6},{6,7},{7,8},{8,9},{9,10},{10,1... | collective-permute-start | bytes 2383880 | tf_op jit(solution)/shard_map/ppermute | solution.py:38
  16.2 52.9 %collective-permute-start.3 = (bf16[1680,256]{1,0:T(8,128)(2,1)}, bf16[1680,256]{1,0:T(8,128)(2,1)S(1)}, u32[]{:S(2)}, u32[]{:S(2)}) collective-permute-start(bf16[1680,256]{1,0:T(8,128)(2,1)} %get-tuple-element.12._), channel_id=1, source_target_pairs={{1,0},{2,1},{3,2},{4,3},{5,4},{6,5},{7,6},{8,7},{9,8},{10,9},{11,1... | collective-permute-start | bytes 2580488 | tf_op jit(solution)/shard_map/ppermute | solution.py:38
  65.0 16.4 %collective-permute-start.6 = (f32[1,128]{1,0:T(1,128)S(1)}, f32[1,128]{1,0:T(1,128)S(1)}, u32[]{:S(2)}, u32[]{:S(2)}) collective-permute-start(f32[1,128]{1,0:T(1,128)S(1)} %bitcast.7), channel_id=1, source_target_pairs={{0,3},{1,2},{2,1},{3,0},{4,7},{5,6},{6,5},{7,4},{8,11},{9,10},{10,... | collective-permute-start | bytes 1544 | tf_op jit(solution)/shard_map/ppermute | solution.py:404
  65.1 16.2 %collective-permute-start.5 = (f32[1,128]{1,0:T(1,128)S(1)}, f32[1,128]{1,0:T(1,128)S(1)}, u32[]{:S(2)}, u32[]{:S(2)}) collective-permute-start(f32[1,128]{1,0:T(1,128)S(1)} %bitcast.8), channel_id=1, source_target_pairs={{0,2},{1,3},{2,0},{3,1},{4,6},{5,7},{6,4},{7,5},{8,10},{9,11},{10,... | collective-permute-start | bytes 1544 | tf_op jit(solution)/shard_map/ppermute | solution.py:404
  65.1 16.2 %collective-permute-start.4 = (f32[1,128]{1,0:T(1,128)S(1)}, f32[1,128]{1,0:T(1,128)S(1)}, u32[]{:S(2)}, u32[]{:S(2)}) collective-permute-start(f32[1,128]{1,0:T(1,128)S(1)} %bitcast.9), channel_id=1, source_target_pairs={{0,1},{1,0},{2,3},{3,2},{4,5},{5,4},{6,7},{7,6},{8,9},{9,8},{10,11... | collective-permute-start | bytes 1544 | tf_op jit(solution)/shard_map/ppermute | solution.py:404

commit v2 on v1

v2 whole, which is shorter than its diff:
```python
import jax
import jax.numpy as jnp
from jax import lax
from jax.experimental import pallas as pl
from jax.experimental.pallas import tpu as pltpu
from jax.sharding import Mesh
from jax.sharding import PartitionSpec as P

GRP_MEM = ("grp_0", "grp_1", "grp_2", "mem")
GRP = ("grp_0", "grp_1", "grp_2")
TILE = 256
HALF = 128
ROWS = 6
BAND = 5
SLOTS = 11
EXTRA = 16
PREFETCH = 600
MIB = 2**20

NEAR = ((1, 5), (2, 5), (3, 4), (3, 5), (4, 5), (3, 3), (4, 4), (5, 5))
FAR = ((1, 2), (1, 3), (1, 4), (2, 3), (2, 4), (1, 1), (2, 2))


def full_of(pairs):
    return [pair for pair in pairs if pair[0] != pair[1]]


def diag_of(pairs):
    return [pair for pair in pairs if pair[0] == pair[1]]


def chunk_rows(pairs):
    return TILE * len(full_of(pairs)) + HALF * len(diag_of(pairs)) + EXTRA


def shift(value, steps):
    count = lax.axis_size(GRP_MEM)
    first, last = max(0, -steps), min(count, count - steps)
    return lax.ppermute(value, GRP_MEM, [(source, source + steps) for source in range(first, last)])


def iotas(shape):
    return lax.broadcasted_iota(jnp.int32, shape, 0), lax.broadcasted_iota(jnp.int32, shape, 1)


def smem():
    return pl.BlockSpec(memory_space=pltpu.SMEM)


def vmem():
    return pl.BlockSpec(memory_space=pltpu.VMEM)


def hbm():
    return pl.BlockSpec(memory_space=pltpu.HBM)


def params(mib):
    return pltpu.CompilerParams(vmem_limit_bytes=mib * MIB)


def cost(products, tiles_moved):
    return pl.CostEstimate(
        flops=2 * TILE**3 * products, bytes_accessed=tiles_moved * TILE * TILE * 2, transcendentals=0
    )


def write_chunk(out, base, pairs, first_row, branch_ref, diag_tile):
    rows, columns = iotas((HALF, HALF))
    extra_rows, _ = iotas((EXTRA, TILE))
    extra = jnp.zeros((EXTRA, TILE), jnp.float32)
    for place, (p, _) in enumerate(diag_of(pairs)):
        tile = diag_tile(p - 1 + first_row)
        low = tile[HALF:, HALF:]
        folded = jnp.where(columns <= rows, tile[:HALF, :HALF], low)
        at = pl.ds(base + place * HALF, HALF)
        out[at, pl.ds(0, HALF)] = tile[HALF:, :HALF].astype(jnp.bfloat16)
        out[at, pl.ds(HALF, HALF)] = folded.astype(jnp.bfloat16)
        line = jnp.sum(jnp.where(columns == rows, low, 0.0), axis=0, keepdims=True)
        line = jnp.concatenate([line, line], axis=1)
        extra = jnp.where(extra_rows == place, line, extra)
    for p in range(1, BAND + 1):
        flag = jnp.where(branch_ref[p - 1 + first_row] == 0, 0.0, 1.0)
        extra = jnp.where(extra_rows == 7 + p, flag, extra)
    out[pl.ds(base + HALF * len(diag_of(pairs)), EXTRA), :] = extra.astype(jnp.bfloat16)


def local_copies(pairs_of_refs, sems):
    copies = [
        pltpu.make_async_copy(source, target, sems.at[number])
        for number, (source, target) in enumerate(pairs_of_refs)
    ]
    for copy in copies:
        copy.start()
    return copies


def pack_corners(tiles, mask, branch, first, last):
    plan = first + last
    diags = [(side, p) for side, (pairs, _) in enumerate(plan) for p, _ in diag_of(pairs)]
    fulls = [(side, place, p, q) for side, (pairs, _) in enumerate(plan) for place, (p, q) in enumerate(full_of(pairs))]
    early = [full for full in fulls if full[0] < len(first)]
    late = [full for full in fulls if full[0] >= len(first)]

    def tail_rows(pairs):
        return HALF * len(diag_of(pairs)) + EXTRA

    def body(mask_hbm, branch_hbm, tiles_ref, *refs):
        outs, refs = refs[: len(plan)], refs[len(plan) :]
        tails, refs = refs[: len(last)], refs[len(last) :]
        mask_ref, branch_ref, diag_ref, zero_ref, table_sems, early_sems, diag_sems, late_sems, tail_sems = refs

        def spot(side, p, q):
            return p - 1 + plan[side][1], q - p + BAND

        tables = local_copies([(mask_hbm, mask_ref), (branch_hbm, branch_ref)], table_sems)
        early_copies = local_copies(
            [
                (tiles_ref.at[spot(side, p, q)], outs[side].at[pl.ds(place * TILE, TILE)])
                for side, place, p, q in early
            ],
            early_sems,
        )
        diag_copies = local_copies(
            [(tiles_ref.at[spot(side, p, p)], diag_ref.at[number]) for number, (side, p) in enumerate(diags)],
            diag_sems,
        )
        zero_ref[...] = jnp.zeros((TILE, TILE), jnp.bfloat16)
        for table in tables:
            table.wait()
        late_copies = []
        for number, (side, place, p, q) in enumerate(late):
            target = outs[side].at[pl.ds(place * TILE, TILE)]
            copy = pltpu.make_async_copy(tiles_ref.at[spot(side, p, q)], target, late_sems.at[number])
            blank = pltpu.make_async_copy(zero_ref, target, late_sems.at[number])
            occupied = mask_ref[spot(side, p, q)] != 0
            pl.when(occupied)(copy.start)
            pl.when(jnp.logical_not(occupied))(blank.start)
            late_copies.append(copy)
        for copy, (side, place, p, q) in zip(early_copies, early):
            copy.wait()

            @pl.when(mask_ref[spot(side, p, q)] == 0)
            def _(out=outs[side], place=place):
                out[pl.ds(place * TILE, TILE), :] = jnp.zeros((TILE, TILE), jnp.bfloat16)

        for copy in diag_copies:
            copy.wait()
        tail_copies = []
        for side, (pairs, first_row) in enumerate(plan):

            def diag_tile(row, side=side, first_row=first_row):
                number = diags.index((side, row + 1 - first_row))
                return diag_ref[number].astype(jnp.float32) * mask_ref[row, BAND].astype(jnp.float32)

            base = TILE * len(full_of(pairs))
            if side < len(first):
                write_chunk(outs[side], base, pairs, first_row, branch_ref, diag_tile)
            else:
                tail = tails[side - len(first)]
                write_chunk(tail, 0, pairs, first_row, branch_ref, diag_tile)
                target = outs[side].at[pl.ds(base, tail_rows(pairs))]
                tail_copies.append(pltpu.make_async_copy(tail, target, tail_sems.at[side - len(first)]))
                tail_copies[-1].start()
        for copy in late_copies + tail_copies:
            copy.wait()

    return pl.pallas_call(
        body,
        out_shape=[
            jax.ShapeDtypeStruct((chunk_rows(pairs), TILE), jnp.bfloat16) for pairs, _ in plan
        ],
        in_specs=[hbm(), hbm(), hbm()],
        out_specs=[vmem() for _ in first] + [hbm() for _ in last],
        scratch_shapes=[pltpu.VMEM((tail_rows(pairs), TILE), jnp.bfloat16) for pairs, _ in last]
        + [
            pltpu.SMEM(mask.shape, mask.dtype),
            pltpu.SMEM(branch.shape, branch.dtype),
            pltpu.VMEM((len(diags), TILE, TILE), jnp.bfloat16),
            pltpu.VMEM((TILE, TILE), jnp.bfloat16),
            pltpu.SemaphoreType.DMA((2,)),
            pltpu.SemaphoreType.DMA((len(early),)),
            pltpu.SemaphoreType.DMA((len(diags),)),
            pltpu.SemaphoreType.DMA((len(late),)),
            pltpu.SemaphoreType.DMA((len(last),)),
        ],
        compiler_params=params(16),
        cost_estimate=cost(PREFETCH, PREFETCH),
        name="pack",
    )(mask, branch, tiles)


def half_scalar(value):
    return value.astype(jnp.float32).astype(jnp.bfloat16)


class Corner:
    def __init__(self, square_ref):
        self.square_ref = square_ref
        self.where = {}
        self.count = 0

    def add(self, chunk, pairs):
        rows, columns = iotas((HALF, HALF))
        for place, pair in enumerate(full_of(pairs)):
            self.where[pair] = (chunk, pl.ds(place * TILE, TILE))
        base = TILE * len(full_of(pairs))
        extra = chunk[pl.ds(base + HALF * len(diag_of(pairs)), EXTRA), :].astype(jnp.float32)
        for place, pair in enumerate(diag_of(pairs)):
            at = pl.ds(base + place * HALF, HALF)
            corner = chunk[at, pl.ds(0, HALF)].astype(jnp.float32)
            folded = chunk[at, pl.ds(HALF, HALF)].astype(jnp.float32)
            turned = folded.T
            line = extra[place : place + 1, :HALF]
            high = jnp.where(columns <= rows, folded, turned)
            low = jnp.where(columns > rows, folded, turned)
            low = jnp.where(columns == rows, line, low)
            target = self.square_ref.at[self.count]
            target[pl.ds(0, HALF), pl.ds(0, HALF)] = high.astype(jnp.bfloat16)
            target[pl.ds(HALF, HALF), pl.ds(HALF, HALF)] = low.astype(jnp.bfloat16)
            target[pl.ds(HALF, HALF), pl.ds(0, HALF)] = corner.astype(jnp.bfloat16)
            target[pl.ds(0, HALF), pl.ds(HALF, HALF)] = corner.T.astype(jnp.bfloat16)
            self.where[pair] = (target, slice(None))
            self.count += 1
        return extra

    def times(self, left, p, q):
        chunk, at = self.where[(min(p, q), max(p, q))]
        return dot(left, chunk[at, :], p > q)


def dot(left, right, transposed):
    return lax.dot_general(
        left, right, (((1,), (1 if transposed else 0,)), ((), ())), preferred_element_type=jnp.float32
    )


def polynomial(square, own, keep, bent):
    return (keep * (1.0 - 2.0 * bent)) * square + (keep * (2.0 * bent)) * own


def squares(value):
    return jnp.sum((value * value).reshape(TILE // 8, 8, TILE), axis=0)


def scalars(mask_ref, branch_ref, row, slot):
    keep = mask_ref[row, slot].astype(jnp.float32)
    bent = jnp.where(branch_ref[row] == 0, 0.0, 1.0)
    return keep, bent


def cross_outputs(up_pairs, down_pairs):
    outputs = []
    for r, q in up_pairs:
        i, j = r - 1, q - 6
        near = [((i, k - i + BAND), (k, j - k + BAND)) for k in range(q)]
        far = [((i, p - 6 - i + BAND), (p, q)) for p in range(r, BAND + 1)]
        outputs.append((i, j - i + BAND, near, far, ("above", q)))
    for r, q in down_pairs:
        i, j = q, 5 + r
        near = [((i, k - i + BAND), (k, j - k + BAND)) for k in range(r, ROWS)]
        far = [((i, 5 + p - i + BAND), (p, r)) for p in range(1, q + 1)]
        outputs.append((i, j - i + BAND, near, far, ("below", r)))
    return outputs


def near_part(tiles_ref, mask_ref, near):
    square = None
    for left, right in near:
        scale = half_scalar(mask_ref[left] * mask_ref[right])
        term = dot(tiles_ref[left] * scale, tiles_ref[right], False)
        square = term if square is None else square + term
    return square


def inner_tiles(tiles, mask, branch, outputs):
    inner = [(i, j) for i in range(ROWS) for j in range(ROWS)]

    def body(mask_ref, branch_ref, tiles_ref, out_ref, sums_ref, parts_ref, new_ref, out_sems):
        rows, columns = iotas((TILE, TILE))
        total = jnp.zeros((8, TILE), jnp.float32)
        trace = jnp.zeros((8, TILE), jnp.float32)
        stores = []

        def emit(i, j, square):
            slot = j - i + BAND
            keep, bent = scalars(mask_ref, branch_ref, i, slot)
            value = polynomial(square, tiles_ref[i, slot].astype(jnp.float32), keep, bent)
            number = i * ROWS + j
            new_ref[number] = value
            stores.append(
                pltpu.make_async_copy(new_ref.at[number], out_ref.at[i, slot], out_sems.at[number])
            )
            stores[-1].start()
            return value

        for i in range(ROWS):
            for j in range(i, ROWS):
                square = None
                for k in range(j - BAND, i + BAND + 1):
                    left, down = (i, k - i + BAND), 0 <= k < ROWS
                    right = (k, j - k + BAND) if down else (j, k - j + BAND)
                    scale = half_scalar(mask_ref[left] * mask_ref[right])
                    term = dot(tiles_ref[left] * scale, tiles_ref[right], not down)
                    square = term if square is None else square + term
                value = emit(i, j, square)
                total = total + squares(value)
                if i == j:
                    part = jnp.where(rows == columns, value, 0.0)
                    trace = trace + jnp.sum(part.reshape(TILE // 8, 8, TILE), axis=0)
                else:
                    total = total + squares(emit(j, i, square.T))
        sums_ref[pl.ds(0, 8), :] = total
        sums_ref[pl.ds(8, 8), :] = trace
        for number, (_, _, near, _, _) in enumerate(outputs):
            parts_ref[number] = near_part(tiles_ref, mask_ref, near)
        for store in stores:
            store.wait()

    products = 196 + sum(len(output[2]) for output in outputs)
    return pl.pallas_call(
        body,
        out_shape=[
            jax.ShapeDtypeStruct((ROWS, SLOTS, TILE, TILE), jnp.float32),
            jax.ShapeDtypeStruct((16, TILE), jnp.float32),
            jax.ShapeDtypeStruct((len(outputs), TILE, TILE), jnp.float32),
        ],
        in_specs=[smem(), smem(), vmem()],
        out_specs=[hbm(), vmem(), vmem()],
        scratch_shapes=[
            pltpu.VMEM((len(inner), TILE, TILE), jnp.float32),
            pltpu.SemaphoreType.DMA((len(inner),)),
        ],
        compiler_params=params(24),
        cost_estimate=cost(products, 66 + 72),
        name="inner",
    )(mask, branch, tiles)


def cross_first(tiles, mask, branch, made, above, below, outputs, parts, sums):
    group = 1
    for axis in GRP:
        group *= lax.axis_size(axis)

    def body(
        mask_ref, branch_ref, tiles_ref, _, above_ref, below_ref, parts_ref, sums_ref,
        out_ref, red_ref, above_square, below_square, new_ref, out_sems,
    ):
        corners = {"above": Corner(above_square), "below": Corner(below_square)}
        flags = {"above": corners["above"].add(above_ref, NEAR), "below": corners["below"].add(below_ref, FAR)}
        total = jnp.zeros((8, TILE), jnp.float32)
        stores = []
        for number, (i, slot, _, far, (side, other)) in enumerate(outputs):
            square = None
            for left, right in far:
                term = corners[side].times(tiles_ref[left] * half_scalar(mask_ref[left]), *right)
                square = term if square is None else square + term
            square = square + parts_ref[number]
            keep, bent = scalars(mask_ref, branch_ref, i, slot)
            mine = tiles_ref[i, slot].astype(jnp.float32)
            value = polynomial(square, mine, keep, bent)
            new_ref[number] = value
            stores.append(
                pltpu.make_async_copy(new_ref.at[number], out_ref.at[i, slot], out_sems.at[number])
            )
            stores[-1].start()
            mirror = polynomial(square, mine, keep, flags[side][7 + other : 8 + other, :])
            total = total + squares(value) + squares(mirror)
        purity = jnp.sum(total + sums_ref[pl.ds(0, 8), :], keepdims=True)
        trace = jnp.sum(sums_ref[pl.ds(8, 8), :], keepdims=True)
        _, lanes = iotas((group, HALF))
        red_ref[...] = jnp.where(lanes == 0, trace, jnp.where(lanes == 1, purity, 0.0))
        for store in stores:
            store.wait()

    return pl.pallas_call(
        body,
        out_shape=[
            jax.ShapeDtypeStruct(made.shape, made.dtype),
            jax.ShapeDtypeStruct((group, HALF), jnp.float32),
        ],
        in_specs=[smem(), smem(), vmem(), hbm(), vmem(), vmem(), vmem(), vmem()],
        out_specs=[hbm(), vmem()],
        scratch_shapes=[
            pltpu.VMEM((len(diag_of(NEAR)), TILE, TILE), jnp.bfloat16),
            pltpu.VMEM((len(diag_of(FAR)), TILE, TILE), jnp.bfloat16),
            pltpu.VMEM((len(outputs), TILE, TILE), jnp.float32),
            pltpu.SemaphoreType.DMA((len(outputs),)),
        ],
        input_output_aliases={3: 0},
        compiler_params=params(16),
        cost_estimate=cost(sum(len(output[3]) for output in outputs), 66 + 2 * len(outputs)),
        name="cross_first",
    )(mask, branch, tiles, made, above, below, parts, sums)


def cross_last(tiles, mask, branch, made, above, below, outputs):
    def body(mask_ref, branch_ref, tiles_ref, _, *refs):
        chunk_refs, (out_ref, above_square, below_square, new_ref, out_sems) = refs[:4], refs[4:]
        corners = {"above": Corner(above_square), "below": Corner(below_square)}
        corners["above"].add(chunk_refs[0], NEAR)
        corners["above"].add(chunk_refs[1], FAR)
        corners["below"].add(chunk_refs[2], FAR)
        corners["below"].add(chunk_refs[3], NEAR)
        stores = []
        for number, output in enumerate(outputs):
            i, slot, near, far, (side, _) = output
            square = near_part(tiles_ref, mask_ref, near)
            for left, right in far:
                square = square + corners[side].times(tiles_ref[left] * half_scalar(mask_ref[left]), *right)
            keep, bent = scalars(mask_ref, branch_ref, i, slot)
            new_ref[number] = polynomial(square, tiles_ref[i, slot].astype(jnp.float32), keep, bent)
            stores.append(
                pltpu.make_async_copy(new_ref.at[number], out_ref.at[i, slot], out_sems.at[number])
            )
            stores[-1].start()
        for store in stores:
            store.wait()

    products = sum(len(output[2]) + len(output[3]) for output in outputs)
    return pl.pallas_call(
        body,
        out_shape=jax.ShapeDtypeStruct(made.shape, made.dtype),
        in_specs=[smem(), smem(), vmem(), hbm()] + [vmem() for _ in range(4)],
        out_specs=hbm(),
        scratch_shapes=[
            pltpu.VMEM((BAND, TILE, TILE), jnp.bfloat16),
            pltpu.VMEM((BAND, TILE, TILE), jnp.bfloat16),
            pltpu.VMEM((len(outputs), TILE, TILE), jnp.float32),
            pltpu.SemaphoreType.DMA((len(outputs),)),
        ],
        input_output_aliases={3: 0},
        compiler_params=params(16),
        cost_estimate=cost(products, 66 + 2 * len(outputs)),
        name="cross_last",
    )(mask, branch, tiles, made, *above, *below)


def add_rows(parts):
    def body(parts_ref, out_ref):
        out_ref[...] = jnp.sum(parts_ref[...], axis=0, keepdims=True)

    return pl.pallas_call(
        body,
        out_shape=jax.ShapeDtypeStruct((1, parts.shape[1]), parts.dtype),
        in_specs=[vmem()],
        out_specs=vmem(),
        compiler_params=params(4),
        cost_estimate=cost(PREFETCH, PREFETCH),
        name="add_rows",
    )(parts)


def on_device(tiles, mask, branch):
    held, mask, branch = (
        pltpu.with_memory_space_constraint(value, pltpu.HBM) for value in (tiles, mask, branch)
    )
    down_first, up_first, down_last, up_last = pack_corners(
        held, mask, branch, ((NEAR, 1), (FAR, 0)), ((FAR, 1), (NEAR, 0))
    )
    above_first, below_first = shift(down_first, 1), shift(up_first, -1)
    above_last = shift(down_last, 1)
    below_last = shift(up_last, -1)
    outputs = cross_outputs(NEAR, FAR)
    made, sums, parts = inner_tiles(tiles, mask, branch, outputs)
    made, part = cross_first(
        tiles, mask, branch, made, above_first, below_first, outputs, parts, sums
    )
    part = add_rows(lax.all_to_all(part, GRP, 0, 0, tiled=True))

    def partner(bits):
        return lax.ppermute(part, "mem", [(m, m ^ bits) for m in range(lax.axis_size("mem"))])

    others = [partner(bits) for bits in (1, 2, 3)]
    part, made = lax.optimization_barrier((part, made))
    made = cross_last(
        tiles,
        mask,
        branch,
        made,
        (above_first, above_last),
        (below_first, below_last),
        cross_outputs(FAR, NEAR),
    )
    traces = (part + others[0]) + (others[1] + others[2])
    order = ROWS * lax.axis_size(GRP_MEM) * TILE
    return made, traces[0, :2] / order


def solution(mesh):
    torus = Mesh(
        mesh.devices.reshape(4, 4, 2, mesh.shape["mem"]), ("grp_0", "grp_1", "grp_2", "mem")
    )
    placed = (P(GRP_MEM, None, None, None), P(GRP_MEM, None), P(GRP_MEM))

    return jax.shard_map(
        on_device,
        mesh=torus,
        in_specs=placed,
        out_specs=(P(GRP_MEM, None, None, None), P()),
        check_vma=False,
    )
```

time: 82.3 us -> 96.2 us (1.17)
  the two profiles are of different devices: /device:TPU:0 before, /device:TPU:7 now
where the time goes in v2:
time: 96.2 us; the launch traced here: 95.9 us
  Pallas kernels  40.8 us (42%)
  starting transfers between devices  33.7 us (35%)
  waiting for transfers between devices  20 us (21%)
    all_to_all x1, starting transfers between devices, on_device(): part = add_rows(lax.all_to_all(part, GRP, 0, 0, tiled=True))  19.8 us
    ppermute x4, waiting for transfers between devices, shift(): lax.ppermute(value, GRP_MEM, [(source, source + steps) for source in rang...  18.3 us
    pallas_call x1, Pallas kernels, pack_corners(): pl.pallas_call(body, out_shape=[jax.ShapeDtypeStruct((chunk_rows(pairs),...  18.2 us
    pallas_call x1, Pallas kernels, inner_tiles(): pl.pallas_call(body, out_shape=[jax.ShapeDtypeStruct((ROWS, SLOTS, TILE,...  11.6 us
    ppermute x4, starting transfers between devices, shift(): lax.ppermute(value, GRP_MEM, [(source, source + steps) for source in rang...  10.6 us
    pallas_call x1, Pallas kernels, cross_last(): pl.pallas_call(body, out_shape=jax.ShapeDtypeStruct(made.shape, made.dtyp...  6.06 us
    pallas_call x1, Pallas kernels, cross_first(): pl.pallas_call(body, out_shape=[jax.ShapeDtypeStruct(made.shape, made.dty...  5.05 us
    ppermute x3, starting transfers between devices, partner(): lax.ppermute(part, 'mem', [(m, m ^ bits) for m in range(lax.axis_size('me...  3.32 us
  transfers between devices with their start and end apart: 8, of which 4 were waited for; matrix products, arithmetic and copies ran while one was open for 0% of the time, Pallas kernels for 18%

profile of v2, /device:TPU:7, one launch (start us, length us, event | category | flops | bytes accessed | tf_op | source)
XLA Modules:
  0.0 95.9 jit_solution(6224824965640335907)
XLA Ops:
  0.6 0.0 copy-start
  0.6 18.2 %pack.1 = (bf16[1680,256]{1,0:T(8,128)(2,1)S(1)}, bf16[1552,256]{1,0:T(8,128)(2,1)S(1)}, bf16[1552,256]{1,0:T(8,128)(2,1)}, bf16[1680,256]{1,0:T(8,128)(2,1)S(1)}) custom-call(s32[6,11]{1,0:T(8,128)} %mask_ref.5, s32[6]{0:T(128)} %branch_ref.5, bf16[6,11,256,256]{3,2,1,0:T(8,128)(2,1)} %tiles_ref.7), custom_call_target="tpu_custom_call" | custom-call | flops 20132659200 | bytes 78643200 | tf_op jit(solution)/shard_map/pack/pallas_call | solution.py:168
  18.8 0.0 copy-start.1
  18.8 1.9 %collective-permute-start = (bf16[1680,256]{1,0:T(8,128)(2,1)S(1)}, bf16[1680,256]{1,0:T(8,128)(2,1)S(1)}, u32[]{:S(2)}, u32[]{:S(2)}) collective-permute-start(bf16[1680,256]{1,0:T(8,128)(2,1)S(1)} %get-tuple-element.14), channel_id=1, source_target_pairs={{0,1},{1,2},{2,3},{3,4},{4,5},{5,6},{6,7},{7,8},{8,9},{9,10},{10,1... | collective-permute-start | bytes 2580488 | tf_op jit(solution)/shard_map/ppermute | solution.py:39
  20.8 0.0 copy-done.1
  20.8 3.4 %collective-permute-start.1 = (bf16[1552,256]{1,0:T(8,128)(2,1)S(1)}, bf16[1552,256]{1,0:T(8,128)(2,1)S(1)}, u32[]{:S(2)}, u32[]{:S(2)}) collective-permute-start(bf16[1552,256]{1,0:T(8,128)(2,1)S(1)} %get-tuple-element.15), channel_id=1, source_target_pairs={{1,0},{2,1},{3,2},{4,3},{5,4},{6,5},{7,6},{8,7},{9,8},{10,9},{11,1... | collective-permute-start | bytes 2383880 | tf_op jit(solution)/shard_map/ppermute | solution.py:39
  24.1 0.0 copy-done
  24.1 11.6 %inner.1 = (f32[6,11,256,256]{3,2,1,0:T(8,128)}, f32[16,256]{1,0:T(8,128)S(1)}, f32[15,256,256]{2,1,0:T(8,128)S(1)}) custom-call(s32[6,11]{1,0:T(8,128)} %mask_ref.5, s32[6]{0:T(128)} %branch_ref.5, bf16[6,11,256,256]{3,2,1,0:T(8,128)(2,1)S(1)} %copy-done), custom_call_target="tpu_custom_call" | custom-call | flops 8858370048 | bytes 18087936 | tf_op jit(solution)/shard_map/inner/pallas_call | solution.py:321
  35.7 1.2 %collective-permute-done.1.below_ref.refs_2_ = bf16[1552,256]{1,0:T(8,128)(2,1)S(1)} collective-permute-done((bf16[1552,256]{1,0:T(8,128)(2,1)S(1)}, bf16[1552,256]{1,0:T(8,128)(2,1)S(1)}, u32[]{:S(2)}, u32[]{:S(2)}) %collective-permute-start.1) | collective-permute-done | bytes 794656 | tf_op jit(solution)/shard_map/ppermute | solution.py:39
  36.9 0.0 collective-permute-done.above_ref.refs_0_
  36.9 0.0 slice-start
  36.9 5.0 %cross_first.1 = (f32[6,11,256,256]{3,2,1,0:T(8,128)}, f32[32,128]{1,0:T(8,128)}) custom-call(s32[6,11]{1,0:T(8,128)} %mask_ref.5, s32[6]{0:T(128)} %branch_ref.5, bf16[6,11,256,256]{3,2,1,0:T(8,128)(2,1)S(1)} %copy-done, f32[6,11,256,256]{3,2,1,0:T(8,128)} %get-tuple-element.13._, ...), custom_call_target="tpu_custom_call", output_to_operand_aliasing={{0}: (3, {})} | custom-call | flops 1409286144 | bytes 12582912 | tf_op jit(solution)/shard_map/cross_first/pallas_call | solution.py:376
  41.9 19.8 %all-to-all-start = ((f32[32,1,128]{2,1,0:T(1,128)}), f32[32,1,128]{2,1,0:T(1,128)S(1)}, u32[]{:S(2)}, u32[]{:S(2)}) async-start(f32[32,1,128]{2,1,0:T(1,128)} %bitcast.1), calls=%async_computation | async-start | bytes 32768 | tf_op jit(solution)/shard_map/all_to_all | solution.py:469
  61.8 2.7 %collective-permute-start.2 = (bf16[1552,256]{1,0:T(8,128)(2,1)}, bf16[1552,256]{1,0:T(8,128)(2,1)}, u32[]{:S(2)}, u32[]{:S(2)}) collective-permute-start(bf16[1552,256]{1,0:T(8,128)(2,1)} %get-tuple-element.21), channel_id=1, source_target_pairs={{0,1},{1,2},{2,3},{3,4},{4,5},{5,6},{6,7},{7,8},{8,9},{9,10},{10,1... | collective-permute-start | bytes 2383880 | tf_op jit(solution)/shard_map/ppermute | solution.py:39
  64.5 2.6 %collective-permute-start.3 = (bf16[1680,256]{1,0:T(8,128)(2,1)}, bf16[1680,256]{1,0:T(8,128)(2,1)S(1)}, u32[]{:S(2)}, u32[]{:S(2)}) collective-permute-start(bf16[1680,256]{1,0:T(8,128)(2,1)} %copy-done.1), channel_id=1, source_target_pairs={{1,0},{2,1},{3,2},{4,3},{5,4},{6,5},{7,6},{8,7},{9,8},{10,9},{11,1... | collective-permute-start | bytes 2580488 | tf_op jit(solution)/shard_map/ppermute | solution.py:39
  67.1 1.7 %all-to-all-done = f32[32,1,128]{2,1,0:T(1,128)S(1)} async-done(((f32[32,1,128]{2,1,0:T(1,128)}), f32[32,1,128]{2,1,0:T(1,128)S(1)}, u32[]{:S(2)}, u32[]{:S(2)}) %all-to-all-start) | async-done | bytes 16416 | tf_op jit(solution)/shard_map/all_to_all | solution.py:469
  68.7 0.0 slice-start.1
  68.7 0.0 slice-start.2
  68.7 0.1 collective-permute-start.6
  68.8 0.2 collective-permute-start.5
  69.0 3.1 %collective-permute-start.4 = (f32[1,128]{1,0:T(1,128)S(1)}, f32[1,128]{1,0:T(1,128)S(1)}, u32[]{:S(2)}, u32[]{:S(2)}) collective-permute-start(f32[1,128]{1,0:T(1,128)S(1)} %add_rows.1), channel_id=1, source_target_pairs={{0,1},{1,0},{2,3},{3,2},{4,5},{5,4},{6,7},{7,6},{8,9},{9,8},{10,11... | collective-permute-start | bytes 1544 | tf_op jit(solution)/shard_map/ppermute | solution.py:472
  72.1 10.9 %collective-permute-done.2.refs_1_ = bf16[1552,256]{1,0:T(8,128)(2,1)} collective-permute-done((bf16[1552,256]{1,0:T(8,128)(2,1)}, bf16[1552,256]{1,0:T(8,128)(2,1)}, u32[]{:S(2)}, u32[]{:S(2)}) %collective-permute-start.2) | collective-permute-done | bytes 794656 | tf_op jit(solution)/shard_map/ppermute | solution.py:39
  83.0 6.2 %collective-permute-done.3.refs_3_ = bf16[1680,256]{1,0:T(8,128)(2,1)S(1)} collective-permute-done((bf16[1680,256]{1,0:T(8,128)(2,1)}, bf16[1680,256]{1,0:T(8,128)(2,1)S(1)}, u32[]{:S(2)}, u32[]{:S(2)}) %collective-permute-start.3) | collective-permute-done | bytes 860192 | tf_op jit(solution)/shard_map/ppermute | solution.py:39
  89.2 0.0 slice-done
  89.2 0.0 slice-done.1
  89.2 0.0 slice-done.2
  89.2 6.1 %cross_last.1 = f32[6,11,256,256]{3,2,1,0:T(8,128)} custom-call(s32[6,11]{1,0:T(8,128)} %mask_ref.5, s32[6]{0:T(128)} %branch_ref.5, bf16[6,11,256,256]{3,2,1,0:T(8,128)(2,1)S(1)} %bitcast.7, f32[6,11,256,256]{3,2,1,0:T(8,128)} %get-tuple-element.20._, bf16[1680,256]{1,0:T(8,128)(2,1)S(1)} %collective-permute-done.above_ref.refs_0_, ...), custom_call_target="tpu_custom_call", output_to_operand_aliasing={{}: (3, {})} | custom-call | flops 3690987520 | bytes 12582912 | tf_op jit(solution)/shard_map/cross_last/pallas_call | solution.py:421
  95.3 0.0 collective-permute-done.6
  95.3 0.0 collective-permute-done.5
  95.3 0.0 collective-permute-done.4
  95.3 0.5 multiply_bitcast_fusion
  (3 shorter events, 0.0 us)
Async XLA Ops:
  0.6 23.5 %copy-start = (bf16[6,11,256,256]{3,2,1,0:T(8,128)(2,1)S(1)}, bf16[6,11,256,256]{3,2,1,0:T(8,128)(2,1)}, u32[]{:S(2)}) copy-start(bf16[6,11,256,256]{3,2,1,0:T(8,128)(2,1)} %tiles_ref.7) | copy-start | bytes 25952260
  18.8 1.9 %copy-start.1 = (bf16[1680,256]{1,0:T(8,128)(2,1)}, bf16[1680,256]{1,0:T(8,128)(2,1)S(1)}, u32[]{:S(2)}) copy-start(bf16[1680,256]{1,0:T(8,128)(2,1)S(1)} %get-tuple-element.22) | copy-start | bytes 2580484
  18.8 18.0 %collective-permute-start = (bf16[1680,256]{1,0:T(8,128)(2,1)S(1)}, bf16[1680,256]{1,0:T(8,128)(2,1)S(1)}, u32[]{:S(2)}, u32[]{:S(2)}) collective-permute-start(bf16[1680,256]{1,0:T(8,128)(2,1)S(1)} %get-tuple-element.14), channel_id=1, source_target_pairs={{0,1},{1,2},{2,3},{3,4},{4,5},{5,6},{6,7},{7,8},{8,9},{9,10},{10,1... | collective-permute-start | bytes 2580488 | tf_op jit(solution)/shard_map/ppermute | solution.py:39
  20.8 16.1 %collective-permute-start.1 = (bf16[1552,256]{1,0:T(8,128)(2,1)S(1)}, bf16[1552,256]{1,0:T(8,128)(2,1)S(1)}, u32[]{:S(2)}, u32[]{:S(2)}) collective-permute-start(bf16[1552,256]{1,0:T(8,128)(2,1)S(1)} %get-tuple-element.15), channel_id=1, source_target_pairs={{1,0},{2,1},{3,2},{4,3},{5,4},{6,5},{7,6},{8,7},{9,8},{10,9},{11,1... | collective-permute-start | bytes 2383880 | tf_op jit(solution)/shard_map/ppermute | solution.py:39
  36.9 52.4 %slice-start = ((s8[8650752]{0:T(1024)(128)(4,1)}), s8[262144]{0:T(1024)(128)(4,1)S(1)}, s32[]{:S(2)}) async-start(s8[8650752]{0:T(1024)(128)(4,1)} %bitcast.6), calls=%async_computation.1 | async-start | bytes 524288
  41.9 26.8 %all-to-all-start = ((f32[32,1,128]{2,1,0:T(1,128)}), f32[32,1,128]{2,1,0:T(1,128)S(1)}, u32[]{:S(2)}, u32[]{:S(2)}) async-start(f32[32,1,128]{2,1,0:T(1,128)} %bitcast.1), calls=%async_computation | async-start | bytes 32768 | tf_op jit(solution)/shard_map/all_to_all | solution.py:469
  61.8 21.3 %collective-permute-start.2 = (bf16[1552,256]{1,0:T(8,128)(2,1)}, bf16[1552,256]{1,0:T(8,128)(2,1)}, u32[]{:S(2)}, u32[]{:S(2)}) collective-permute-start(bf16[1552,256]{1,0:T(8,128)(2,1)} %get-tuple-element.21), channel_id=1, source_target_pairs={{0,1},{1,2},{2,3},{3,4},{4,5},{5,6},{6,7},{7,8},{8,9},{9,10},{10,1... | collective-permute-start | bytes 2383880 | tf_op jit(solution)/shard_map/ppermute | solution.py:39
  64.5 24.7 %collective-permute-start.3 = (bf16[1680,256]{1,0:T(8,128)(2,1)}, bf16[1680,256]{1,0:T(8,128)(2,1)S(1)}, u32[]{:S(2)}, u32[]{:S(2)}) collective-permute-start(bf16[1680,256]{1,0:T(8,128)(2,1)} %copy-done.1), channel_id=1, source_target_pairs={{1,0},{2,1},{3,2},{4,3},{5,4},{6,5},{7,6},{8,7},{9,8},{10,9},{11,1... | collective-permute-start | bytes 2580488 | tf_op jit(solution)/shard_map/ppermute | solution.py:39
  68.7 20.5 %slice-start.1 = ((s8[8650752]{0:T(1024)(128)(4,1)}), s8[4194304]{0:T(1024)(128)(4,1)S(1)}, s32[]{:S(2)}) async-start(s8[8650752]{0:T(1024)(128)(4,1)} %bitcast.6), calls=%async_computation.2 | async-start | bytes 8388608
  68.7 20.5 %slice-start.2 = ((s8[8650752]{0:T(1024)(128)(4,1)}), s8[4194304]{0:T(1024)(128)(4,1)S(1)}, s32[]{:S(2)}) async-start(s8[8650752]{0:T(1024)(128)(4,1)} %bitcast.6), calls=%async_computation.3 | async-start | bytes 8388608
  68.7 26.6 %collective-permute-start.6 = (f32[1,128]{1,0:T(1,128)S(1)}, f32[1,128]{1,0:T(1,128)S(1)}, u32[]{:S(2)}, u32[]{:S(2)}) collective-permute-start(f32[1,128]{1,0:T(1,128)S(1)} %add_rows.1), channel_id=1, source_target_pairs={{0,3},{1,2},{2,1},{3,0},{4,7},{5,6},{6,5},{7,4},{8,11},{9,10},{10,... | collective-permute-start | bytes 1544 | tf_op jit(solution)/shard_map/ppermute | solution.py:472
  68.8 26.5 %collective-permute-start.5 = (f32[1,128]{1,0:T(1,128)S(1)}, f32[1,128]{1,0:T(1,128)S(1)}, u32[]{:S(2)}, u32[]{:S(2)}) collective-permute-start(f32[1,128]{1,0:T(1,128)S(1)} %add_rows.1), channel_id=1, source_target_pairs={{0,2},{1,3},{2,0},{3,1},{4,6},{5,7},{6,4},{7,5},{8,10},{9,11},{10,... | collective-permute-start | bytes 1544 | tf_op jit(solution)/shard_map/ppermute | solution.py:472
  69.0 26.3 %collective-permute-start.4 = (f32[1,128]{1,0:T(1,128)S(1)}, f32[1,128]{1,0:T(1,128)S(1)}, u32[]{:S(2)}, u32[]{:S(2)}) collective-permute-start(f32[1,128]{1,0:T(1,128)S(1)} %add_rows.1), channel_id=1, source_target_pairs={{0,1},{1,0},{2,3},{3,2},{4,5},{5,4},{6,7},{7,6},{8,9},{9,8},{10,11... | collective-permute-start | bytes 1544 | tf_op jit(solution)/shard_map/ppermute | solution.py:472

commit v3 on v2

v3 whole, which is shorter than its diff:
```python
import jax
import jax.numpy as jnp
from jax import lax
from jax.experimental import pallas as pl
from jax.experimental.pallas import tpu as pltpu
from jax.sharding import Mesh
from jax.sharding import PartitionSpec as P

GRP_MEM = ("grp_0", "grp_1", "grp_2", "mem")
GRP = ("grp_0", "grp_1", "grp_2")
TILE = 256
HALF = 128
ROWS = 6
BAND = 5
SLOTS = 11
EXTRA = 16
PREFETCH = 600
MIB = 2**20

NEAR = ((1, 5), (2, 5), (3, 4), (3, 5), (4, 5), (3, 3), (4, 4), (5, 5))
FAR = ((1, 2), (1, 3), (1, 4), (2, 3), (2, 4), (1, 1), (2, 2))


def full_of(pairs):
    return [pair for pair in pairs if pair[0] != pair[1]]


def diag_of(pairs):
    return [pair for pair in pairs if pair[0] == pair[1]]


def chunk_rows(pairs):
    return TILE * len(full_of(pairs)) + HALF * len(diag_of(pairs)) + EXTRA


def shift(value, steps):
    count = lax.axis_size(GRP_MEM)
    first, last = max(0, -steps), min(count, count - steps)
    return lax.ppermute(value, GRP_MEM, [(source, source + steps) for source in range(first, last)])


def iotas(shape):
    return lax.broadcasted_iota(jnp.int32, shape, 0), lax.broadcasted_iota(jnp.int32, shape, 1)


def smem():
    return pl.BlockSpec(memory_space=pltpu.SMEM)


def vmem():
    return pl.BlockSpec(memory_space=pltpu.VMEM)


def hbm():
    return pl.BlockSpec(memory_space=pltpu.HBM)


def params(mib):
    return pltpu.CompilerParams(vmem_limit_bytes=mib * MIB)


def cost(products, tiles_moved):
    return pl.CostEstimate(
        flops=2 * TILE**3 * products, bytes_accessed=tiles_moved * TILE * TILE * 2, transcendentals=0
    )


def write_chunk(out, pairs, first_row, branch_ref, diag_tile):
    rows, columns = iotas((HALF, HALF))
    extra_rows, _ = iotas((EXTRA, TILE))
    base = TILE * len(full_of(pairs))
    extra = jnp.zeros((EXTRA, TILE), jnp.float32)
    for place, (p, _) in enumerate(diag_of(pairs)):
        tile = diag_tile(p - 1 + first_row)
        low = tile[HALF:, HALF:]
        folded = jnp.where(columns <= rows, tile[:HALF, :HALF], low)
        at = pl.ds(base + place * HALF, HALF)
        out[at, pl.ds(0, HALF)] = tile[HALF:, :HALF].astype(jnp.bfloat16)
        out[at, pl.ds(HALF, HALF)] = folded.astype(jnp.bfloat16)
        line = jnp.sum(jnp.where(columns == rows, low, 0.0), axis=0, keepdims=True)
        line = jnp.concatenate([line, line], axis=1)
        extra = jnp.where(extra_rows == place, line, extra)
    for p in range(1, BAND + 1):
        flag = jnp.where(branch_ref[p - 1 + first_row] == 0, 0.0, 1.0)
        extra = jnp.where(extra_rows == 7 + p, flag, extra)
    out[pl.ds(base + HALF * len(diag_of(pairs)), EXTRA), :] = extra.astype(jnp.bfloat16)


def chunk_shapes(plan):
    return [jax.ShapeDtypeStruct((chunk_rows(pairs), TILE), jnp.bfloat16) for pairs, _ in plan]


def local_copies(pairs_of_refs, sems):
    copies = [
        pltpu.make_async_copy(source, target, sems.at[number])
        for number, (source, target) in enumerate(pairs_of_refs)
    ]
    for copy in copies:
        copy.start()
    return copies


def pack_corners(tiles, mask, branch, plan):
    diags = [(side, p) for side, (pairs, _) in enumerate(plan) for p, _ in diag_of(pairs)]
    fulls = [
        (side, place, p, q)
        for side, (pairs, _) in enumerate(plan)
        for place, (p, q) in enumerate(full_of(pairs))
    ]

    def body(mask_hbm, branch_hbm, tiles_ref, *refs):
        outs, refs = refs[: len(plan)], refs[len(plan) :]
        mask_ref, branch_ref, diag_ref, table_sems, full_sems, diag_sems = refs

        def spot(side, p, q):
            return p - 1 + plan[side][1], q - p + BAND

        tables = local_copies([(mask_hbm, mask_ref), (branch_hbm, branch_ref)], table_sems)
        diag_copies = local_copies(
            [(tiles_ref.at[spot(side, p, p)], diag_ref.at[number]) for number, (side, p) in enumerate(diags)],
            diag_sems,
        )
        full_copies = local_copies(
            [
                (tiles_ref.at[spot(side, p, q)], outs[side].at[pl.ds(place * TILE, TILE)])
                for side, place, p, q in fulls
            ],
            full_sems,
        )
        for copy in tables + diag_copies:
            copy.wait()
        for side, (pairs, first_row) in enumerate(plan):

            def diag_tile(row, side=side, first_row=first_row):
                number = diags.index((side, row + 1 - first_row))
                return diag_ref[number].astype(jnp.float32) * mask_ref[row, BAND].astype(jnp.float32)

            write_chunk(outs[side], pairs, first_row, branch_ref, diag_tile)
        for copy, (side, place, p, q) in zip(full_copies, fulls):
            copy.wait()

            @pl.when(mask_ref[spot(side, p, q)] == 0)
            def _(out=outs[side], place=place):
                out[pl.ds(place * TILE, TILE), :] = jnp.zeros((TILE, TILE), jnp.bfloat16)

    return pl.pallas_call(
        body,
        out_shape=chunk_shapes(plan),
        in_specs=[hbm(), hbm(), hbm()],
        out_specs=[vmem() for _ in plan],
        scratch_shapes=[
            pltpu.SMEM(mask.shape, mask.dtype),
            pltpu.SMEM(branch.shape, branch.dtype),
            pltpu.VMEM((len(diags), TILE, TILE), jnp.bfloat16),
            pltpu.SemaphoreType.DMA((2,)),
            pltpu.SemaphoreType.DMA((len(fulls),)),
            pltpu.SemaphoreType.DMA((len(diags),)),
        ],
        compiler_params=params(16),
        cost_estimate=cost(PREFETCH, PREFETCH),
        name="pack",
    )(mask, branch, tiles)


def half_scalar(value):
    return value.astype(jnp.float32).astype(jnp.bfloat16)


class Corner:
    def __init__(self, square_ref):
        self.square_ref = square_ref
        self.where = {}
        self.count = 0

    def add(self, chunk, pairs):
        rows, columns = iotas((HALF, HALF))
        for place, pair in enumerate(full_of(pairs)):
            self.where[pair] = (chunk, pl.ds(place * TILE, TILE))
        base = TILE * len(full_of(pairs))
        extra = chunk[pl.ds(base + HALF * len(diag_of(pairs)), EXTRA), :].astype(jnp.float32)
        for place, pair in enumerate(diag_of(pairs)):
            at = pl.ds(base + place * HALF, HALF)
            corner = chunk[at, pl.ds(0, HALF)].astype(jnp.float32)
            folded = chunk[at, pl.ds(HALF, HALF)].astype(jnp.float32)
            turned = folded.T
            line = extra[place : place + 1, :HALF]
            high = jnp.where(columns <= rows, folded, turned)
            low = jnp.where(columns > rows, folded, turned)
            low = jnp.where(columns == rows, line, low)
            target = self.square_ref.at[self.count]
            target[pl.ds(0, HALF), pl.ds(0, HALF)] = high.astype(jnp.bfloat16)
            target[pl.ds(HALF, HALF), pl.ds(HALF, HALF)] = low.astype(jnp.bfloat16)
            target[pl.ds(HALF, HALF), pl.ds(0, HALF)] = corner.astype(jnp.bfloat16)
            target[pl.ds(0, HALF), pl.ds(HALF, HALF)] = corner.T.astype(jnp.bfloat16)
            self.where[pair] = (target, slice(None))
            self.count += 1
        return extra

    def times(self, left, p, q):
        chunk, at = self.where[(min(p, q), max(p, q))]
        return dot(left, chunk[at, :], p > q)


def dot(left, right, transposed):
    return lax.dot_general(
        left, right, (((1,), (1 if transposed else 0,)), ((), ())), preferred_element_type=jnp.float32
    )


def polynomial(square, own, keep, bent):
    return (keep * (1.0 - 2.0 * bent)) * square + (keep * (2.0 * bent)) * own


def squares(value):
    return jnp.sum((value * value).reshape(TILE // 8, 8, TILE), axis=0)


def scalars(mask_ref, branch_ref, row, slot):
    keep = mask_ref[row, slot].astype(jnp.float32)
    bent = jnp.where(branch_ref[row] == 0, 0.0, 1.0)
    return keep, bent


def cross_outputs(up_pairs, down_pairs):
    outputs = []
    for r, q in up_pairs:
        i, j = r - 1, q - 6
        near = [((i, k - i + BAND), (k, j - k + BAND)) for k in range(q)]
        far = [((i, p - 6 - i + BAND), (p, q)) for p in range(r, BAND + 1)]
        outputs.append((i, j - i + BAND, near, far, ("above", q)))
    for r, q in down_pairs:
        i, j = q, 5 + r
        near = [((i, k - i + BAND), (k, j - k + BAND)) for k in range(r, ROWS)]
        far = [((i, 5 + p - i + BAND), (p, r)) for p in range(1, q + 1)]
        outputs.append((i, j - i + BAND, near, far, ("below", r)))
    return outputs


def near_part(tiles_ref, mask_ref, near):
    square = None
    for left, right in near:
        scale = half_scalar(mask_ref[left] * mask_ref[right])
        term = dot(tiles_ref[left] * scale, tiles_ref[right], False)
        square = term if square is None else square + term
    return square


def inner_tiles(tiles, mask, branch, outputs, plan):
    inner = [(i, j) for i in range(ROWS) for j in range(ROWS)]

    def body(mask_ref, branch_ref, tiles_ref, out_ref, sums_ref, parts_ref, *refs):
        chunks, (new_ref, out_sems) = refs[: len(plan)], refs[len(plan) :]
        rows, columns = iotas((TILE, TILE))
        total = jnp.zeros((8, TILE), jnp.float32)
        trace = jnp.zeros((8, TILE), jnp.float32)
        stores = []
        pending = []

        def emit(i, j, square):
            slot = j - i + BAND
            keep, bent = scalars(mask_ref, branch_ref, i, slot)
            value = polynomial(square, tiles_ref[i, slot].astype(jnp.float32), keep, bent)
            number = i * ROWS + j
            new_ref[number] = value
            pending.append(
                pltpu.make_async_copy(new_ref.at[number], out_ref.at[i, slot], out_sems.at[number])
            )
            return value

        def send():
            for copy in pending:
                copy.start()
            stores.extend(pending)
            pending.clear()

        def finish(i, j, square, total, trace):
            value = emit(i, j, square)
            total = total + squares(value)
            if i == j:
                part = jnp.where(rows == columns, value, 0.0)
                trace = trace + jnp.sum(part.reshape(TILE // 8, 8, TILE), axis=0)
            else:
                total = total + squares(emit(j, i, square.T))
            return total, trace

        waiting = None
        for i, j in [(i, j) for i in range(ROWS) for j in range(i, ROWS)]:
            square = None
            for k in range(j - BAND, i + BAND + 1):
                left, down = (i, k - i + BAND), 0 <= k < ROWS
                right = (k, j - k + BAND) if down else (j, k - j + BAND)
                scale = half_scalar(mask_ref[left] * mask_ref[right])
                term = dot(tiles_ref[left] * scale, tiles_ref[right], not down)
                square = term if square is None else square + term
            if waiting is not None:
                total, trace = finish(*waiting, total, trace)
            if len(pending) > GROUP:
                send()
            waiting = (i, j, square)
        total, trace = finish(*waiting, total, trace)
        send()
        sums_ref[pl.ds(0, 8), :] = total
        sums_ref[pl.ds(8, 8), :] = trace
        for number, (_, _, near, _, _) in enumerate(outputs):
            parts_ref[number] = near_part(tiles_ref, mask_ref, near)
        for (pairs, first_row), out in zip(plan, chunks):
            for place, (p, q) in enumerate(full_of(pairs)):
                spot = p - 1 + first_row, q - p + BAND
                out[pl.ds(place * TILE, TILE), :] = tiles_ref[spot] * half_scalar(mask_ref[spot])

            def diag_tile(row):
                return tiles_ref[row, BAND].astype(jnp.float32) * mask_ref[row, BAND].astype(jnp.float32)

            write_chunk(out, pairs, first_row, branch_ref, diag_tile)
        for store in stores:
            store.wait()

    products = 196 + sum(len(output[2]) for output in outputs)
    return pl.pallas_call(
        body,
        out_shape=[
            jax.ShapeDtypeStruct((ROWS, SLOTS, TILE, TILE), jnp.float32),
            jax.ShapeDtypeStruct((16, TILE), jnp.float32),
            jax.ShapeDtypeStruct((len(outputs), TILE, TILE), jnp.float32),
        ]
        + chunk_shapes(plan),
        in_specs=[smem(), smem(), vmem()],
        out_specs=[hbm()] + [vmem() for _ in range(2 + len(plan))],
        scratch_shapes=[
            pltpu.VMEM((len(inner), TILE, TILE), jnp.float32),
            pltpu.SemaphoreType.DMA((len(inner),)),
        ],
        compiler_params=params(24),
        cost_estimate=cost(products, 66 + 72),
        name="inner",
    )(mask, branch, tiles)


def table_shapes(mask, branch):
    return [
        pltpu.SMEM(mask.shape, mask.dtype),
        pltpu.SMEM(branch.shape, branch.dtype),
        pltpu.SemaphoreType.DMA((2,)),
    ]


def cross_first(tiles, mask, branch, above, below, outputs, parts, sums):
    group = 1
    for axis in GRP:
        group *= lax.axis_size(axis)

    def body(
        mask_hbm, branch_hbm, tiles_ref, above_ref, below_ref, parts_ref, sums_ref,
        new_ref, red_ref, mask_ref, branch_ref, table_sems, above_square, below_square,
    ):
        tables = local_copies([(mask_hbm, mask_ref), (branch_hbm, branch_ref)], table_sems)
        corners = {"above": Corner(above_square), "below": Corner(below_square)}
        flags = {"above": corners["above"].add(above_ref, NEAR), "below": corners["below"].add(below_ref, FAR)}
        for table in tables:
            table.wait()
        total = jnp.zeros((8, TILE), jnp.float32)

        def finish(number, square, total):
            i, slot, _, _, (side, other) = outputs[number]
            square = square + parts_ref[number]
            keep, bent = scalars(mask_ref, branch_ref, i, slot)
            mine = tiles_ref[i, slot].astype(jnp.float32)
            value = polynomial(square, mine, keep, bent)
            new_ref[number] = value
            mirror = polynomial(square, mine, keep, flags[side][7 + other : 8 + other, :])
            return total + squares(value) + squares(mirror)

        waiting = None
        for number, (_, _, _, far, (side, _)) in enumerate(outputs):
            square = None
            for left, right in far:
                term = corners[side].times(tiles_ref[left] * half_scalar(mask_ref[left]), *right)
                square = term if square is None else square + term
            if waiting is not None:
                total = finish(*waiting, total)
            waiting = (number, square)
        total = finish(*waiting, total)
        purity = jnp.sum(total + sums_ref[pl.ds(0, 8), :], keepdims=True)
        trace = jnp.sum(sums_ref[pl.ds(8, 8), :], keepdims=True)
        _, lanes = iotas((group, HALF))
        red_ref[...] = jnp.where(lanes == 0, trace, jnp.where(lanes == 1, purity, 0.0))

    return pl.pallas_call(
        body,
        out_shape=[
            jax.ShapeDtypeStruct((len(outputs), TILE, TILE), jnp.float32),
            jax.ShapeDtypeStruct((group, HALF), jnp.float32),
        ],
        in_specs=[hbm(), hbm(), vmem(), vmem(), vmem(), vmem(), vmem()],
        out_specs=[vmem(), vmem()],
        scratch_shapes=table_shapes(mask, branch)
        + [
            pltpu.VMEM((len(diag_of(NEAR)), TILE, TILE), jnp.bfloat16),
            pltpu.VMEM((len(diag_of(FAR)), TILE, TILE), jnp.bfloat16),
        ],
        compiler_params=params(16),
        cost_estimate=cost(sum(len(output[3]) for output in outputs), 66 + 2 * len(outputs)),
        name="cross_first",
    )(mask, branch, tiles, above, below, parts, sums)


GROUP = 4


def cross_last(tiles, mask, branch, made, above, below, outputs, ready_outputs, ready):
    def body(mask_hbm, branch_hbm, tiles_ref, _, ready_ref, *refs):
        chunk_refs, refs = refs[:4], refs[4:]
        (
            out_ref, mask_ref, branch_ref, table_sems, above_square, below_square, new_ref, out_sems, ready_sems,
        ) = refs
        tables = local_copies([(mask_hbm, mask_ref), (branch_hbm, branch_ref)], table_sems)
        stores = local_copies(
            [
                (ready_ref.at[number], out_ref.at[i, slot])
                for number, (i, slot, *_) in enumerate(ready_outputs)
            ],
            ready_sems,
        )
        corners = {"above": Corner(above_square), "below": Corner(below_square)}
        corners["above"].add(chunk_refs[0], NEAR)
        corners["above"].add(chunk_refs[1], FAR)
        corners["below"].add(chunk_refs[2], FAR)
        corners["below"].add(chunk_refs[3], NEAR)
        for table in tables:
            table.wait()

        def finish(number, square):
            i, slot = outputs[number][:2]
            keep, bent = scalars(mask_ref, branch_ref, i, slot)
            new_ref[number] = polynomial(square, tiles_ref[i, slot].astype(jnp.float32), keep, bent)

        def send(numbers):
            for number in numbers:
                i, slot = outputs[number][:2]
                stores.append(
                    pltpu.make_async_copy(new_ref.at[number], out_ref.at[i, slot], out_sems.at[number])
                )
                stores[-1].start()

        waiting = None
        for number, (_, _, near, far, (side, _)) in enumerate(outputs):
            square = near_part(tiles_ref, mask_ref, near)
            for left, right in far:
                square = square + corners[side].times(tiles_ref[left] * half_scalar(mask_ref[left]), *right)
            if waiting is not None:
                finish(*waiting)
            if number and number % GROUP == 0:
                send(range(number - GROUP, number))
            waiting = (number, square)
        finish(*waiting)
        send(range((len(outputs) - 1) // GROUP * GROUP, len(outputs)))
        for store in stores:
            store.wait()

    products = sum(len(output[2]) + len(output[3]) for output in outputs)
    return pl.pallas_call(
        body,
        out_shape=jax.ShapeDtypeStruct(made.shape, made.dtype),
        in_specs=[hbm(), hbm(), vmem(), hbm(), vmem()] + [vmem() for _ in range(4)],
        out_specs=hbm(),
        scratch_shapes=table_shapes(mask, branch)
        + [
            pltpu.VMEM((BAND, TILE, TILE), jnp.bfloat16),
            pltpu.VMEM((BAND, TILE, TILE), jnp.bfloat16),
            pltpu.VMEM((len(outputs), TILE, TILE), jnp.float32),
            pltpu.SemaphoreType.DMA((len(outputs),)),
            pltpu.SemaphoreType.DMA((len(ready_outputs),)),
        ],
        input_output_aliases={3: 0},
        compiler_params=params(16),
        cost_estimate=cost(products, 66 + 2 * len(outputs)),
        name="cross_last",
    )(mask, branch, tiles, made, ready, *above, *below)


def add_rows(parts):
    def body(parts_ref, out_ref):
        out_ref[...] = jnp.sum(parts_ref[...], axis=0, keepdims=True)

    return pl.pallas_call(
        body,
        out_shape=jax.ShapeDtypeStruct((1, parts.shape[1]), parts.dtype),
        in_specs=[vmem()],
        out_specs=vmem(),
        compiler_params=params(4),
        cost_estimate=cost(PREFETCH, PREFETCH),
        name="add_rows",
    )(parts)


def on_device(tiles, mask, branch):
    held, mask, branch = (
        pltpu.with_memory_space_constraint(value, pltpu.HBM) for value in (tiles, mask, branch)
    )
    down_first, up_first = pack_corners(held, mask, branch, ((NEAR, 1), (FAR, 0)))
    above_first, below_first = shift(down_first, 1), shift(up_first, -1)
    outputs = cross_outputs(NEAR, FAR)
    made, sums, parts, down_last, up_last = inner_tiles(
        tiles, mask, branch, outputs, ((FAR, 1), (NEAR, 0))
    )
    above_last = shift(down_last, 1)
    below_last = shift(up_last, -1)
    ready, part = cross_first(tiles, mask, branch, above_first, below_first, outputs, parts, sums)
    part = add_rows(lax.all_to_all(part, GRP, 0, 0, tiled=True))

    def partner(bits):
        return lax.ppermute(part, "mem", [(m, m ^ bits) for m in range(lax.axis_size("mem"))])

    others = [partner(bits) for bits in (1, 2, 3)]
    part, made = lax.optimization_barrier((part, made))
    made = cross_last(
        tiles,
        mask,
        branch,
        made,
        (above_first, above_last),
        (below_first, below_last),
        cross_outputs(FAR, NEAR),
        outputs,
        ready,
    )
    traces = (part + others[0]) + (others[1] + others[2])
    order = ROWS * lax.axis_size(GRP_MEM) * TILE
    return made, traces[0, :2] / order


def solution(mesh):
    torus = Mesh(
        mesh.devices.reshape(4, 4, 2, mesh.shape["mem"]), ("grp_0", "grp_1", "grp_2", "mem")
    )
    placed = (P(GRP_MEM, None, None, None), P(GRP_MEM, None), P(GRP_MEM))

    return jax.shard_map(
        on_device,
        mesh=torus,
        in_specs=placed,
        out_specs=(P(GRP_MEM, None, None, None), P()),
        check_vma=False,
    )
```

time: 96.2 us -> 78.3 us (0.81)
  Pallas kernels: 40.8 us -> 25.4 us
  starting transfers between devices: 33.7 us -> 22.4 us
  waiting for transfers between devices: 20 us -> 27.1 us
  local copies, waits for them, and re-layouts: 0.02 us -> 1.87 us
    pallas_call x2, Pallas kernels: 23.2 us -> 6.15 us  [the longest x1 4.06 us: cross_first(): pl.pallas_call(body, out_shape=[jax.ShapeDtypeStruct((len(outputs), TILE,...]
    all_to_all x1, starting transfers between devices: 19.8 us -> 7.91 us  [on_device(): part = add_rows(lax.all_to_all(part, GRP, 0, 0, tiled=True))]
    ppermute x4, waiting for transfers between devices: 18.3 us -> 25.4 us  [shift(): lax.ppermute(value, GRP_MEM, [(source, source + steps) for source in rang...]
    unnamed x10 -> x14, local copies, waits for them, and re-layouts: 0.02 us -> 1.87 us
    pallas_call x1, Pallas kernels: 6.06 us -> 7.05 us  [cross_last(): pl.pallas_call(body, out_shape=jax.ShapeDtypeStruct(made.shape, made.dtyp...]
  transfers between devices with their start and end apart: 8 -> 8, of which waited for: 4 -> 4; matrix products, arithmetic and copies ran while one was open for 0% -> 0% of each run, Pallas kernels for 18% -> 25%
where the time goes in v3:
time: 78.3 us; the launch traced here: 78 us
  waiting for transfers between devices  27.1 us (35%)
  Pallas kernels  25.4 us (32%)
  starting transfers between devices  22.4 us (29%)
  local copies, waits for them, and re-layouts  1.87 us (2%)
  between operations  0.81 us (1%)
    ppermute x4, waiting for transfers between devices, shift(): lax.ppermute(value, GRP_MEM, [(source, source + steps) for source in rang...  25.4 us
    pallas_call x1, Pallas kernels, inner_tiles(): pl.pallas_call(body, out_shape=[jax.ShapeDtypeStruct((ROWS, SLOTS, TILE,...  12.2 us
    ppermute x4, starting transfers between devices, shift(): lax.ppermute(value, GRP_MEM, [(source, source + steps) for source in rang...  11.1 us
    all_to_all x1, starting transfers between devices, on_device(): part = add_rows(lax.all_to_all(part, GRP, 0, 0, tiled=True))  7.91 us
    pallas_call x1, Pallas kernels, cross_last(): pl.pallas_call(body, out_shape=jax.ShapeDtypeStruct(made.shape, made.dtyp...  7.05 us
    pallas_call x1, Pallas kernels, cross_first(): pl.pallas_call(body, out_shape=[jax.ShapeDtypeStruct((len(outputs), TILE,...  4.06 us
    ppermute x3, starting transfers between devices, partner(): lax.ppermute(part, 'mem', [(m, m ^ bits) for m in range(lax.axis_size('me...  3.32 us
    pallas_call x1, Pallas kernels, pack_corners(): pl.pallas_call(body, out_shape=chunk_shapes(plan), in_specs=[hbm(), hbm()...  2.09 us
  transfers between devices with their start and end apart: 8, of which 4 were waited for; matrix products, arithmetic and copies ran while one was open for 0% of the time, Pallas kernels for 25%

profile of v3, /device:TPU:7, one launch (start us, length us, event | category | flops | bytes accessed | tf_op | source)
XLA Modules:
  0.0 78.0 jit_solution(12592336861137418438)
XLA Ops:
  0.6 0.0 copy-start
  0.6 2.1 %pack.1 = (bf16[1680,256]{1,0:T(8,128)(2,1)S(1)}, bf16[1552,256]{1,0:T(8,128)(2,1)S(1)}) custom-call(s32[6,11]{1,0:T(8,128)} %mask_hbm.5, s32[6]{0:T(128)} %branch_hbm.5, bf16[6,11,256,256]{3,2,1,0:T(8,128)(2,1)} %tiles_ref.7), custom_call_target="tpu_custom_call" | custom-call | flops 20132659200 | bytes 78643200 | tf_op jit(solution)/shard_map/pack/pallas_call | solution.py:146
  2.7 3.9 %collective-permute-start = (bf16[1680,256]{1,0:T(8,128)(2,1)S(1)}, bf16[1680,256]{1,0:T(8,128)(2,1)S(1)}, u32[]{:S(2)}, u32[]{:S(2)}) collective-permute-start(bf16[1680,256]{1,0:T(8,128)(2,1)S(1)} %get-tuple-element.13), channel_id=1, source_target_pairs={{0,1},{1,2},{2,3},{3,4},{4,5},{5,6},{6,7},{7,8},{8,9},{9,10},{10,1... | collective-permute-start | bytes 2580488 | tf_op jit(solution)/shard_map/ppermute | solution.py:39
  6.7 1.9 %collective-permute-start.1 = (bf16[1552,256]{1,0:T(8,128)(2,1)S(1)}, bf16[1552,256]{1,0:T(8,128)(2,1)S(1)}, u32[]{:S(2)}, u32[]{:S(2)}) collective-permute-start(bf16[1552,256]{1,0:T(8,128)(2,1)S(1)} %get-tuple-element.14), channel_id=1, source_target_pairs={{1,0},{2,1},{3,2},{4,3},{5,4},{6,5},{7,6},{8,7},{9,8},{10,9},{11,1... | collective-permute-start | bytes 2383880 | tf_op jit(solution)/shard_map/ppermute | solution.py:39
  8.6 0.0 copy-done
  8.6 12.2 %inner.1 = (f32[6,11,256,256]{3,2,1,0:T(8,128)}, f32[16,256]{1,0:T(8,128)S(1)}, f32[15,256,256]{2,1,0:T(8,128)S(1)}, bf16[1552,256]{1,0:T(8,128)(2,1)}, bf16[1680,256]{1,0:T(8,128)(2,1)S(1)}) custom-call(s32[6,11]{1,0:T(8,128)} %mask_hbm.5, s32[6]{0:T(128)} %branch_hbm.5, bf16[6,11,256,256]{3,2,1,0:T(8,128)(2,1)S(1)} %copy-done), custom_call_target="tpu_custom_call" | custom-call | flops 8858370048 | bytes 18087936 | tf_op jit(solution)/shard_map/inner/pallas_call | solution.py:319
  20.8 0.0 copy-start.3
  20.8 8.2 %collective-permute-done.1.below_ref.refs_2_ = bf16[1552,256]{1,0:T(8,128)(2,1)S(1)} collective-permute-done((bf16[1552,256]{1,0:T(8,128)(2,1)S(1)}, bf16[1552,256]{1,0:T(8,128)(2,1)S(1)}, u32[]{:S(2)}, u32[]{:S(2)}) %collective-permute-start.1) | collective-permute-done | bytes 794656 | tf_op jit(solution)/shard_map/ppermute | solution.py:39
  29.0 0.0 collective-permute-done.above_ref.refs_0_
  29.1 0.0 slice-start
  29.1 4.1 %cross_first.1 = (f32[15,256,256]{2,1,0:T(8,128)S(1)}, f32[32,128]{1,0:T(8,128)}) custom-call(s32[6,11]{1,0:T(8,128)} %mask_hbm.5, s32[6]{0:T(128)} %branch_hbm.5, bf16[6,11,256,256]{3,2,1,0:T(8,128)(2,1)S(1)} %copy-done, bf16[1680,256]{1,0:T(8,128)(2,1)S(1)} %collective-permute-done.above_ref.refs_0_, ...), custom_call_target="tpu_custom_call" | custom-call | flops 1409286144 | bytes 12582912 | tf_op jit(solution)/shard_map/cross_first/pallas_call | solution.py:388
  33.1 0.0 copy-done.3
  33.1 0.0 copy-start.1
  33.1 1.8 %copy-done.1 = f32[15,256,256]{2,1,0:T(8,128)} copy-done((f32[15,256,256]{2,1,0:T(8,128)}, f32[15,256,256]{2,1,0:T(8,128)S(1)}, u32[]{:S(2)}) %copy-start.1) | copy-done | bytes 3932184
  35.0 7.9 %all-to-all-start = ((f32[32,1,128]{2,1,0:T(1,128)}), f32[32,1,128]{2,1,0:T(1,128)S(1)}, u32[]{:S(2)}, u32[]{:S(2)}) async-start(f32[32,1,128]{2,1,0:T(1,128)} %bitcast.1), calls=%async_computation | async-start | bytes 32768 | tf_op jit(solution)/shard_map/all_to_all | solution.py:509
  42.9 2.9 %collective-permute-start.2 = (bf16[1552,256]{1,0:T(8,128)(2,1)}, bf16[1552,256]{1,0:T(8,128)(2,1)}, u32[]{:S(2)}, u32[]{:S(2)}) collective-permute-start(bf16[1552,256]{1,0:T(8,128)(2,1)} %get-tuple-element.21), channel_id=1, source_target_pairs={{0,1},{1,2},{2,3},{3,4},{4,5},{5,6},{6,7},{7,8},{8,9},{9,10},{10,1... | collective-permute-start | bytes 2383880 | tf_op jit(solution)/shard_map/ppermute | solution.py:39
  45.8 2.4 %collective-permute-start.3 = (bf16[1680,256]{1,0:T(8,128)(2,1)}, bf16[1680,256]{1,0:T(8,128)(2,1)S(1)}, u32[]{:S(2)}, u32[]{:S(2)}) collective-permute-start(bf16[1680,256]{1,0:T(8,128)(2,1)} %copy-done.3), channel_id=1, source_target_pairs={{1,0},{2,1},{3,2},{4,3},{5,4},{6,5},{7,6},{8,7},{9,8},{10,9},{11,1... | collective-permute-start | bytes 2580488 | tf_op jit(solution)/shard_map/ppermute | solution.py:39
  48.2 1.7 %all-to-all-done = f32[32,1,128]{2,1,0:T(1,128)S(1)} async-done(((f32[32,1,128]{2,1,0:T(1,128)}), f32[32,1,128]{2,1,0:T(1,128)S(1)}, u32[]{:S(2)}, u32[]{:S(2)}) %all-to-all-start) | async-done | bytes 16416 | tf_op jit(solution)/shard_map/all_to_all | solution.py:509
  49.9 0.1 collective-permute-start.6
  50.0 1.3 %collective-permute-start.5 = (f32[1,128]{1,0:T(1,128)S(1)}, f32[1,128]{1,0:T(1,128)S(1)}, u32[]{:S(2)}, u32[]{:S(2)}) collective-permute-start(f32[1,128]{1,0:T(1,128)S(1)} %add_rows.1), channel_id=1, source_target_pairs={{0,2},{1,3},{2,0},{3,1},{4,6},{5,7},{6,4},{7,5},{8,10},{9,11},{10,... | collective-permute-start | bytes 1544 | tf_op jit(solution)/shard_map/ppermute | solution.py:512
  51.3 1.9 %collective-permute-start.4 = (f32[1,128]{1,0:T(1,128)S(1)}, f32[1,128]{1,0:T(1,128)S(1)}, u32[]{:S(2)}, u32[]{:S(2)}) collective-permute-start(f32[1,128]{1,0:T(1,128)S(1)} %add_rows.1), channel_id=1, source_target_pairs={{0,1},{1,0},{2,3},{3,2},{4,5},{5,4},{6,7},{7,6},{8,9},{9,8},{10,11... | collective-permute-start | bytes 1544 | tf_op jit(solution)/shard_map/ppermute | solution.py:512
  53.2 10.9 %collective-permute-done.2.refs_1_ = bf16[1552,256]{1,0:T(8,128)(2,1)} collective-permute-done((bf16[1552,256]{1,0:T(8,128)(2,1)}, bf16[1552,256]{1,0:T(8,128)(2,1)}, u32[]{:S(2)}, u32[]{:S(2)}) %collective-permute-start.2) | collective-permute-done | bytes 794656 | tf_op jit(solution)/shard_map/ppermute | solution.py:39
  64.2 6.2 %collective-permute-done.3.refs_3_ = bf16[1680,256]{1,0:T(8,128)(2,1)S(1)} collective-permute-done((bf16[1680,256]{1,0:T(8,128)(2,1)}, bf16[1680,256]{1,0:T(8,128)(2,1)S(1)}, u32[]{:S(2)}, u32[]{:S(2)}) %collective-permute-start.3) | collective-permute-done | bytes 860192 | tf_op jit(solution)/shard_map/ppermute | solution.py:39
  70.4 0.0 slice-done
  70.4 0.0 slice-done.1
  70.4 0.0 slice-done.2
  70.4 0.0 copy-done.2
  70.4 7.0 %cross_last.1 = f32[6,11,256,256]{3,2,1,0:T(8,128)} custom-call(s32[6,11]{1,0:T(8,128)} %mask_hbm.5, s32[6]{0:T(128)} %branch_hbm.5, bf16[6,11,256,256]{3,2,1,0:T(8,128)(2,1)S(1)} %bitcast.7, f32[6,11,256,256]{3,2,1,0:T(8,128)} %get-tuple-element.19._, f32[15,256,256]{2,1,0:T(8,128)S(1)} %copy-done.2, ...), custom_call_target="tpu_custom_call", output_to_operand_aliasing={{}: (3, {})} | custom-call | flops 3690987520 | bytes 12582912 | tf_op jit(solution)/shard_map/cross_last/pallas_call | solution.py:461
  77.4 0.0 collective-permute-done.6
  77.5 0.0 collective-permute-done.5
  77.5 0.0 collective-permute-done.4
  77.5 0.5 multiply_bitcast_fusion
  (6 shorter events, 0.0 us)
Async XLA Ops:
  0.6 8.0 %copy-start = (bf16[6,11,256,256]{3,2,1,0:T(8,128)(2,1)S(1)}, bf16[6,11,256,256]{3,2,1,0:T(8,128)(2,1)}, u32[]{:S(2)}) copy-start(bf16[6,11,256,256]{3,2,1,0:T(8,128)(2,1)} %tiles_ref.7) | copy-start | bytes 25952260
  2.7 26.3 %collective-permute-start = (bf16[1680,256]{1,0:T(8,128)(2,1)S(1)}, bf16[1680,256]{1,0:T(8,128)(2,1)S(1)}, u32[]{:S(2)}, u32[]{:S(2)}) collective-permute-start(bf16[1680,256]{1,0:T(8,128)(2,1)S(1)} %get-tuple-element.13), channel_id=1, source_target_pairs={{0,1},{1,2},{2,3},{3,4},{4,5},{5,6},{6,7},{7,8},{8,9},{9,10},{10,1... | collective-permute-start | bytes 2580488 | tf_op jit(solution)/shard_map/ppermute | solution.py:39
  6.7 22.4 %collective-permute-start.1 = (bf16[1552,256]{1,0:T(8,128)(2,1)S(1)}, bf16[1552,256]{1,0:T(8,128)(2,1)S(1)}, u32[]{:S(2)}, u32[]{:S(2)}) collective-permute-start(bf16[1552,256]{1,0:T(8,128)(2,1)S(1)} %get-tuple-element.14), channel_id=1, source_target_pairs={{1,0},{2,1},{3,2},{4,3},{5,4},{6,5},{7,6},{8,7},{9,8},{10,9},{11,1... | collective-permute-start | bytes 2383880 | tf_op jit(solution)/shard_map/ppermute | solution.py:39
  20.8 12.3 %copy-start.3 = (bf16[1680,256]{1,0:T(8,128)(2,1)}, bf16[1680,256]{1,0:T(8,128)(2,1)S(1)}, u32[]{:S(2)}) copy-start(bf16[1680,256]{1,0:T(8,128)(2,1)S(1)} %get-tuple-element.22) | copy-start | bytes 2580484
  29.1 41.3 %slice-start = ((s8[8650752]{0:T(1024)(128)(4,1)}), s8[262144]{0:T(1024)(128)(4,1)S(1)}, s32[]{:S(2)}) async-start(s8[8650752]{0:T(1024)(128)(4,1)} %bitcast.6), calls=%async_computation.1 | async-start | bytes 524288
  33.1 1.9 %copy-start.1 = (f32[15,256,256]{2,1,0:T(8,128)}, f32[15,256,256]{2,1,0:T(8,128)S(1)}, u32[]{:S(2)}) copy-start(f32[15,256,256]{2,1,0:T(8,128)S(1)} %get-tuple-element.20.ready_ref) | copy-start | bytes 11796484
  35.0 14.9 %all-to-all-start = ((f32[32,1,128]{2,1,0:T(1,128)}), f32[32,1,128]{2,1,0:T(1,128)S(1)}, u32[]{:S(2)}, u32[]{:S(2)}) async-start(f32[32,1,128]{2,1,0:T(1,128)} %bitcast.1), calls=%async_computation | async-start | bytes 32768 | tf_op jit(solution)/shard_map/all_to_all | solution.py:509
  42.9 21.3 %collective-permute-start.2 = (bf16[1552,256]{1,0:T(8,128)(2,1)}, bf16[1552,256]{1,0:T(8,128)(2,1)}, u32[]{:S(2)}, u32[]{:S(2)}) collective-permute-start(bf16[1552,256]{1,0:T(8,128)(2,1)} %get-tuple-element.21), channel_id=1, source_target_pairs={{0,1},{1,2},{2,3},{3,4},{4,5},{5,6},{6,7},{7,8},{8,9},{9,10},{10,1... | collective-permute-start | bytes 2383880 | tf_op jit(solution)/shard_map/ppermute | solution.py:39
  45.8 24.6 %collective-permute-start.3 = (bf16[1680,256]{1,0:T(8,128)(2,1)}, bf16[1680,256]{1,0:T(8,128)(2,1)S(1)}, u32[]{:S(2)}, u32[]{:S(2)}) collective-permute-start(bf16[1680,256]{1,0:T(8,128)(2,1)} %copy-done.3), channel_id=1, source_target_pairs={{1,0},{2,1},{3,2},{4,3},{5,4},{6,5},{7,6},{8,7},{9,8},{10,9},{11,1... | collective-permute-start | bytes 2580488 | tf_op jit(solution)/shard_map/ppermute | solution.py:39
  49.9 20.5 %slice-start.1 = ((s8[8650752]{0:T(1024)(128)(4,1)}), s8[4194304]{0:T(1024)(128)(4,1)S(1)}, s32[]{:S(2)}) async-start(s8[8650752]{0:T(1024)(128)(4,1)} %bitcast.6), calls=%async_computation.2 | async-start | bytes 8388608
  49.9 20.5 %slice-start.2 = ((s8[8650752]{0:T(1024)(128)(4,1)}), s8[4194304]{0:T(1024)(128)(4,1)S(1)}, s32[]{:S(2)}) async-start(s8[8650752]{0:T(1024)(128)(4,1)} %bitcast.6), calls=%async_computation.3 | async-start | bytes 8388608
  49.9 20.5 %copy-start.2 = (f32[15,256,256]{2,1,0:T(8,128)S(1)}, f32[15,256,256]{2,1,0:T(8,128)}, u32[]{:S(2)}) copy-start(f32[15,256,256]{2,1,0:T(8,128)} %copy-done.1) | copy-start | bytes 11796484
  49.9 27.6 %collective-permute-start.6 = (f32[1,128]{1,0:T(1,128)S(1)}, f32[1,128]{1,0:T(1,128)S(1)}, u32[]{:S(2)}, u32[]{:S(2)}) collective-permute-start(f32[1,128]{1,0:T(1,128)S(1)} %add_rows.1), channel_id=1, source_target_pairs={{0,3},{1,2},{2,1},{3,0},{4,7},{5,6},{6,5},{7,4},{8,11},{9,10},{10,... | collective-permute-start | bytes 1544 | tf_op jit(solution)/shard_map/ppermute | solution.py:512
  50.0 27.5 %collective-permute-start.5 = (f32[1,128]{1,0:T(1,128)S(1)}, f32[1,128]{1,0:T(1,128)S(1)}, u32[]{:S(2)}, u32[]{:S(2)}) collective-permute-start(f32[1,128]{1,0:T(1,128)S(1)} %add_rows.1), channel_id=1, source_target_pairs={{0,2},{1,3},{2,0},{3,1},{4,6},{5,7},{6,4},{7,5},{8,10},{9,11},{10,... | collective-permute-start | bytes 1544 | tf_op jit(solution)/shard_map/ppermute | solution.py:512
  51.3 26.2 %collective-permute-start.4 = (f32[1,128]{1,0:T(1,128)S(1)}, f32[1,128]{1,0:T(1,128)S(1)}, u32[]{:S(2)}, u32[]{:S(2)}) collective-permute-start(f32[1,128]{1,0:T(1,128)S(1)} %add_rows.1), channel_id=1, source_target_pairs={{0,1},{1,0},{2,3},{3,2},{4,5},{5,4},{6,7},{7,6},{8,9},{9,8},{10,11... | collective-permute-start | bytes 1544 | tf_op jit(solution)/shard_map/ppermute | solution.py:512

commit v4 on v3

--- a/solution.py
+++ b/solution.py
@@ -33,10 +33,20 @@
     return TILE * len(full_of(pairs)) + HALF * len(diag_of(pairs)) + EXTRA
 
 
-def shift(value, steps):
-    count = lax.axis_size(GRP_MEM)
-    first, last = max(0, -steps), min(count, count - steps)
-    return lax.ppermute(value, GRP_MEM, [(source, source + steps) for source in range(first, last)])
+CHUNK = max(chunk_rows(NEAR), chunk_rows(FAR))
+
+
+def swap(value, first):
+    pairs = []
+    for low in range(first, lax.axis_size(GRP_MEM) - 1, 2):
+        pairs += [(low, low + 1), (low + 1, low)]
+    return lax.ppermute(value, GRP_MEM, pairs)
+
+
+def by_parity(act):
+    odd = lax.axis_index("mem") % 2
+    pl.when(odd == 0)(lambda: act(True))
+    pl.when(odd == 1)(lambda: act(False))
 
 
 def iotas(shape):
@@ -87,7 +97,7 @@
 
 
 def chunk_shapes(plan):
-    return [jax.ShapeDtypeStruct((chunk_rows(pairs), TILE), jnp.bfloat16) for pairs, _ in plan]
+    return [jax.ShapeDtypeStruct((CHUNK, TILE), jnp.bfloat16) for _ in plan]
 
 
 def local_copies(pairs_of_refs, sems):
@@ -109,7 +119,11 @@
     ]
 
     def body(mask_hbm, branch_hbm, tiles_ref, *refs):
+        by_parity(lambda even: run(even, mask_hbm, branch_hbm, tiles_ref, *refs))
+
+    def run(even, mask_hbm, branch_hbm, tiles_ref, *refs):
         outs, refs = refs[: len(plan)], refs[len(plan) :]
+        outs = outs if even else outs[::-1]
         mask_ref, branch_ref, diag_ref, table_sems, full_sems, diag_sems = refs
 
         def spot(side, p, q):
@@ -303,15 +317,18 @@
         sums_ref[pl.ds(8, 8), :] = trace
         for number, (_, _, near, _, _) in enumerate(outputs):
             parts_ref[number] = near_part(tiles_ref, mask_ref, near)
-        for (pairs, first_row), out in zip(plan, chunks):
-            for place, (p, q) in enumerate(full_of(pairs)):
-                spot = p - 1 + first_row, q - p + BAND
-                out[pl.ds(place * TILE, TILE), :] = tiles_ref[spot] * half_scalar(mask_ref[spot])
-
-            def diag_tile(row):
-                return tiles_ref[row, BAND].astype(jnp.float32) * mask_ref[row, BAND].astype(jnp.float32)
-
-            write_chunk(out, pairs, first_row, branch_ref, diag_tile)
+
+        def diag_tile(row):
+            return tiles_ref[row, BAND].astype(jnp.float32) * mask_ref[row, BAND].astype(jnp.float32)
+
+        def pack(even):
+            for (pairs, first_row), out in zip(plan, chunks if even else chunks[::-1]):
+                for place, (p, q) in enumerate(full_of(pairs)):
+                    spot = p - 1 + first_row, q - p + BAND
+                    out[pl.ds(place * TILE, TILE), :] = tiles_ref[spot] * half_scalar(mask_ref[spot])
+                write_chunk(out, pairs, first_row, branch_ref, diag_tile)
+
+        by_parity(pack)
         for store in stores:
             store.wait()
 
@@ -336,6 +353,14 @@
     )(mask, branch, tiles)
 
 
+def sort_sides(first_ref, second_ref, above_ref, below_ref):
+    def copy(even):
+        above_ref[...] = (second_ref if even else first_ref)[...]
+        below_ref[...] = (first_ref if even else second_ref)[...]
+
+    by_parity(copy)
+
+
 def table_shapes(mask, branch):
     return [
         pltpu.SMEM(mask.shape, mask.dtype),
@@ -344,16 +369,17 @@
     ]
 
 
-def cross_first(tiles, mask, branch, above, below, outputs, parts, sums):
+def cross_first(tiles, mask, branch, swaps, outputs, parts, sums):
     group = 1
     for axis in GRP:
         group *= lax.axis_size(axis)
 
     def body(
-        mask_hbm, branch_hbm, tiles_ref, above_ref, below_ref, parts_ref, sums_ref,
-        new_ref, red_ref, mask_ref, branch_ref, table_sems, above_square, below_square,
+        mask_hbm, branch_hbm, tiles_ref, first_ref, second_ref, parts_ref, sums_ref,
+        new_ref, red_ref, above_ref, below_ref, mask_ref, branch_ref, table_sems, above_square, below_square,
     ):
         tables = local_copies([(mask_hbm, mask_ref), (branch_hbm, branch_ref)], table_sems)
+        sort_sides(first_ref, second_ref, above_ref, below_ref)
         corners = {"above": Corner(above_square), "below": Corner(below_square)}
         flags = {"above": corners["above"].add(above_ref, NEAR), "below": corners["below"].add(below_ref, FAR)}
         for table in tables:
@@ -390,9 +416,11 @@
         out_shape=[
             jax.ShapeDtypeStruct((len(outputs), TILE, TILE), jnp.float32),
             jax.ShapeDtypeStruct((group, HALF), jnp.float32),
+            jax.ShapeDtypeStruct((CHUNK, TILE), jnp.bfloat16),
+            jax.ShapeDtypeStruct((CHUNK, TILE), jnp.bfloat16),
         ],
         in_specs=[hbm(), hbm(), vmem(), vmem(), vmem(), vmem(), vmem()],
-        out_specs=[vmem(), vmem()],
+        out_specs=[vmem() for _ in range(4)],
         scratch_shapes=table_shapes(mask, branch)
         + [
             pltpu.VMEM((len(diag_of(NEAR)), TILE, TILE), jnp.bfloat16),
@@ -401,17 +429,18 @@
         compiler_params=params(16),
         cost_estimate=cost(sum(len(output[3]) for output in outputs), 66 + 2 * len(outputs)),
         name="cross_first",
-    )(mask, branch, tiles, above, below, parts, sums)
+    )(mask, branch, tiles, *swaps, parts, sums)
 
 
 GROUP = 4
 
 
-def cross_last(tiles, mask, branch, made, above, below, outputs, ready_outputs, ready):
+def cross_last(tiles, mask, branch, made, sides, swaps, outputs, ready_outputs, ready):
     def body(mask_hbm, branch_hbm, tiles_ref, _, ready_ref, *refs):
         chunk_refs, refs = refs[:4], refs[4:]
         (
-            out_ref, mask_ref, branch_ref, table_sems, above_square, below_square, new_ref, out_sems, ready_sems,
+            out_ref, mask_ref, branch_ref, table_sems, above_ref, below_ref, above_square, below_square, new_ref,
+            out_sems, ready_sems,
         ) = refs
         tables = local_copies([(mask_hbm, mask_ref), (branch_hbm, branch_ref)], table_sems)
         stores = local_copies(
@@ -422,10 +451,11 @@
             ready_sems,
         )
         corners = {"above": Corner(above_square), "below": Corner(below_square)}
+        sort_sides(chunk_refs[2], chunk_refs[3], above_ref, below_ref)
         corners["above"].add(chunk_refs[0], NEAR)
-        corners["above"].add(chunk_refs[1], FAR)
-        corners["below"].add(chunk_refs[2], FAR)
-        corners["below"].add(chunk_refs[3], NEAR)
+        corners["above"].add(above_ref, FAR)
+        corners["below"].add(chunk_refs[1], FAR)
+        corners["below"].add(below_ref, NEAR)
         for table in tables:
             table.wait()
 
@@ -465,6 +495,8 @@
         out_specs=hbm(),
         scratch_shapes=table_shapes(mask, branch)
         + [
+            pltpu.VMEM((CHUNK, TILE), jnp.bfloat16),
+            pltpu.VMEM((CHUNK, TILE), jnp.bfloat16),
             pltpu.VMEM((BAND, TILE, TILE), jnp.bfloat16),
             pltpu.VMEM((BAND, TILE, TILE), jnp.bfloat16),
             pltpu.VMEM((len(outputs), TILE, TILE), jnp.float32),
@@ -475,7 +507,7 @@
         compiler_params=params(16),
         cost_estimate=cost(products, 66 + 2 * len(outputs)),
         name="cross_last",
-    )(mask, branch, tiles, made, ready, *above, *below)
+    )(mask, branch, tiles, made, ready, *sides, *swaps)
 
 
 def add_rows(parts):
@@ -497,15 +529,16 @@
     held, mask, branch = (
         pltpu.with_memory_space_constraint(value, pltpu.HBM) for value in (tiles, mask, branch)
     )
-    down_first, up_first = pack_corners(held, mask, branch, ((NEAR, 1), (FAR, 0)))
-    above_first, below_first = shift(down_first, 1), shift(up_first, -1)
+    packed = pack_corners(held, mask, branch, ((NEAR, 1), (FAR, 0)))
+    swaps_first = [swap(packed[0], 0)]
+    swaps_first.append(swap(packed[1], 1))
     outputs = cross_outputs(NEAR, FAR)
-    made, sums, parts, down_last, up_last = inner_tiles(
+    made, sums, parts, *packed = inner_tiles(
         tiles, mask, branch, outputs, ((FAR, 1), (NEAR, 0))
     )
-    above_last = shift(down_last, 1)
-    below_last = shift(up_last, -1)
-    ready, part = cross_first(tiles, mask, branch, above_first, below_first, outputs, parts, sums)
+    swaps_last = [swap(packed[0], 0)]
+    swaps_last.append(swap(packed[1], 1))
+    ready, part, *sides = cross_first(tiles, mask, branch, swaps_first, outputs, parts, sums)
     part = add_rows(lax.all_to_all(part, GRP, 0, 0, tiled=True))
 
     def partner(bits):
@@ -518,8 +551,8 @@
         mask,
         branch,
         made,
-        (above_first, above_last),
-        (below_first, below_last),
+        sides,
+        swaps_last,
         cross_outputs(FAR, NEAR),
         outputs,
         ready,

time: 78.3 us -> 78.1 us (level)
  the two profiles are of different devices: /device:TPU:7 before, /device:TPU:32 now
where the time goes in v4:
time: 78.1 us; the launch traced here: 77.8 us
  waiting for transfers between devices  26.6 us (34%)
  Pallas kernels  24.4 us (31%)
  starting transfers between devices  23.5 us (30%)
  local copies, waits for them, and re-layouts  1.89 us (2%)
  between operations  0.83 us (1%)
    ppermute x4, waiting for transfers between devices, swap(): return lax.ppermute(value, GRP_MEM, pairs)  26.6 us
    ppermute x4, starting transfers between devices, swap(): return lax.ppermute(value, GRP_MEM, pairs)  13.1 us
    pallas_call x1, Pallas kernels, inner_tiles(): pl.pallas_call(body, out_shape=[jax.ShapeDtypeStruct((ROWS, SLOTS, TILE,...  11.2 us
    pallas_call x1, Pallas kernels, cross_last(): pl.pallas_call(body, out_shape=jax.ShapeDtypeStruct(made.shape, made.dtyp...  7.02 us
    all_to_all x1, starting transfers between devices, on_device(): part = add_rows(lax.all_to_all(part, GRP, 0, 0, tiled=True))  6.22 us
    ppermute x3, starting transfers between devices, partner(): lax.ppermute(part, 'mem', [(m, m ^ bits) for m in range(lax.axis_size('me...  4.17 us
    pallas_call x1, Pallas kernels, cross_first(): pl.pallas_call(body, out_shape=[jax.ShapeDtypeStruct((len(outputs), TILE,...  4.13 us
    pallas_call x1, Pallas kernels, pack_corners(): pl.pallas_call(body, out_shape=chunk_shapes(plan), in_specs=[hbm(), hbm()...  2.09 us
  transfers between devices with their start and end apart: 8, of which 4 were waited for; matrix products, arithmetic and copies ran while one was open for 0% of the time, Pallas kernels for 23%

profile of v4, /device:TPU:32, one launch (start us, length us, event | category | flops | bytes accessed | tf_op | source)
XLA Modules:
  0.0 77.8 jit_solution(8520759549073209402)
XLA Ops:
  0.6 0.0 copy-start
  0.6 2.1 %pack.1 = (bf16[1680,256]{1,0:T(8,128)(2,1)S(1)}, bf16[1680,256]{1,0:T(8,128)(2,1)S(1)}) custom-call(s32[6,11]{1,0:T(8,128)} %mask_hbm.5, s32[6]{0:T(128)} %branch_hbm.5, bf16[6,11,256,256]{3,2,1,0:T(8,128)(2,1)} %tiles_ref.7), custom_call_target="tpu_custom_call" | custom-call | flops 20132659200 | bytes 78643200 | tf_op jit(solution)/shard_map/pack/pallas_call | solution.py:160
  2.7 1.6 %collective-permute-start = (bf16[1680,256]{1,0:T(8,128)(2,1)S(1)}, bf16[1680,256]{1,0:T(8,128)(2,1)S(1)}, u32[]{:S(2)}, u32[]{:S(2)}) collective-permute-start(bf16[1680,256]{1,0:T(8,128)(2,1)S(1)} %get-tuple-element.15), channel_id=1, source_target_pairs={{0,1},{1,0},{2,3},{3,2},{4,5},{5,4},{6,7},{7,6},{8,9},{9,8},{10,11... | collective-permute-start | bytes 2580488 | tf_op jit(solution)/shard_map/ppermute | solution.py:43
  4.3 5.3 %collective-permute-start.1 = (bf16[1680,256]{1,0:T(8,128)(2,1)S(1)}, bf16[1680,256]{1,0:T(8,128)(2,1)S(1)}, u32[]{:S(2)}, u32[]{:S(2)}) collective-permute-start(bf16[1680,256]{1,0:T(8,128)(2,1)S(1)} %get-tuple-element.16), channel_id=1, source_target_pairs={{1,2},{2,1},{3,4},{4,3},{5,6},{6,5},{7,8},{8,7},{9,10},{10,9},{11,... | collective-permute-start | bytes 2580488 | tf_op jit(solution)/shard_map/ppermute | solution.py:43
  9.6 0.0 copy-done
  9.6 11.2 %inner.1 = (f32[6,11,256,256]{3,2,1,0:T(8,128)}, f32[16,256]{1,0:T(8,128)S(1)}, f32[15,256,256]{2,1,0:T(8,128)S(1)}, bf16[1680,256]{1,0:T(8,128)(2,1)S(1)}, bf16[1680,256]{1,0:T(8,128)(2,1)S(1)}) custom-call(s32[6,11]{1,0:T(8,128)} %mask_hbm.5, s32[6]{0:T(128)} %branch_hbm.5, bf16[6,11,256,256]{3,2,1,0:T(8,128)(2,1)S(1)} %copy-done), custom_call_target="tpu_custom_call" | custom-call | flops 8858370048 | bytes 18087936 | tf_op jit(solution)/shard_map/inner/pallas_call | solution.py:336
  20.8 0.0 copy-start.3
  20.8 0.0 copy-start.4
  20.8 2.8 %collective-permute-done.first_ref = bf16[1680,256]{1,0:T(8,128)(2,1)S(1)} collective-permute-done((bf16[1680,256]{1,0:T(8,128)(2,1)S(1)}, bf16[1680,256]{1,0:T(8,128)(2,1)S(1)}, u32[]{:S(2)}, u32[]{:S(2)}) %collective-permute-start) | collective-permute-done | bytes 860192 | tf_op jit(solution)/shard_map/ppermute | solution.py:43
  23.7 6.9 %collective-permute-done.1.second_ref = bf16[1680,256]{1,0:T(8,128)(2,1)S(1)} collective-permute-done((bf16[1680,256]{1,0:T(8,128)(2,1)S(1)}, bf16[1680,256]{1,0:T(8,128)(2,1)S(1)}, u32[]{:S(2)}, u32[]{:S(2)}) %collective-permute-start.1) | collective-permute-done | bytes 860192 | tf_op jit(solution)/shard_map/ppermute | solution.py:43
  30.6 4.1 %cross_first.1 = (f32[15,256,256]{2,1,0:T(8,128)S(1)}, f32[32,128]{1,0:T(8,128)}, bf16[1680,256]{1,0:T(8,128)(2,1)S(1)}, bf16[1680,256]{1,0:T(8,128)(2,1)S(1)}) custom-call(s32[6,11]{1,0:T(8,128)} %mask_hbm.5, s32[6]{0:T(128)} %branch_hbm.5, bf16[6,11,256,256]{3,2,1,0:T(8,128)(2,1)S(1)} %copy-done, bf16[1680,256]{1,0:T(8,128)(2,1)S(1)} %collective-permute-done.first_ref, ...), custom_call_target="tpu_custom_call" | custom-call | flops 1409286144 | bytes 12582912 | tf_op jit(solution)/shard_map/cross_first/pallas_call | solution.py:414
  34.7 1.9 %copy-done.1 = f32[15,256,256]{2,1,0:T(8,128)} copy-done((f32[15,256,256]{2,1,0:T(8,128)}, f32[15,256,256]{2,1,0:T(8,128)S(1)}, u32[]{:S(2)}) %copy-start.1) | copy-done | bytes 3932184
  36.6 0.0 copy-done.4
  36.6 6.2 %all-to-all-start = ((f32[32,1,128]{2,1,0:T(1,128)}), f32[32,1,128]{2,1,0:T(1,128)S(1)}, u32[]{:S(2)}, u32[]{:S(2)}) async-start(f32[32,1,128]{2,1,0:T(1,128)} %bitcast.1), calls=%async_computation | async-start | bytes 32768 | tf_op jit(solution)/shard_map/all_to_all | solution.py:542
  42.8 0.1 collective-permute-start.2
  42.9 6.2 %collective-permute-start.3 = (bf16[1680,256]{1,0:T(8,128)(2,1)}, bf16[1680,256]{1,0:T(8,128)(2,1)}, u32[]{:S(2)}, u32[]{:S(2)}) collective-permute-start(bf16[1680,256]{1,0:T(8,128)(2,1)} %copy-done.3), channel_id=1, source_target_pairs={{1,2},{2,1},{3,4},{4,3},{5,6},{6,5},{7,8},{8,7},{9,10},{10,9},{11,... | collective-permute-start | bytes 2580488 | tf_op jit(solution)/shard_map/ppermute | solution.py:43
  49.1 0.0 all-to-all-done
  49.1 0.0 slice-start.1
  49.1 0.0 slice-start.2
  49.1 0.0 copy-start.2
  49.1 2.4 %collective-permute-start.6 = (f32[1,128]{1,0:T(1,128)S(1)}, f32[1,128]{1,0:T(1,128)S(1)}, u32[]{:S(2)}, u32[]{:S(2)}) collective-permute-start(f32[1,128]{1,0:T(1,128)S(1)} %add_rows.1), channel_id=1, source_target_pairs={{0,3},{1,2},{2,1},{3,0},{4,7},{5,6},{6,5},{7,4},{8,11},{9,10},{10,... | collective-permute-start | bytes 1544 | tf_op jit(solution)/shard_map/ppermute | solution.py:545
  51.5 0.0 collective-permute-start.5
  51.5 1.8 %collective-permute-start.4 = (f32[1,128]{1,0:T(1,128)S(1)}, f32[1,128]{1,0:T(1,128)S(1)}, u32[]{:S(2)}, u32[]{:S(2)}) collective-permute-start(f32[1,128]{1,0:T(1,128)S(1)} %add_rows.1), channel_id=1, source_target_pairs={{0,1},{1,0},{2,3},{3,2},{4,5},{5,4},{6,7},{7,6},{8,9},{9,8},{10,11... | collective-permute-start | bytes 1544 | tf_op jit(solution)/shard_map/ppermute | solution.py:545
  53.3 10.9 %collective-permute-done.2.refs_2_ = bf16[1680,256]{1,0:T(8,128)(2,1)S(1)} collective-permute-done((bf16[1680,256]{1,0:T(8,128)(2,1)}, bf16[1680,256]{1,0:T(8,128)(2,1)S(1)}, u32[]{:S(2)}, u32[]{:S(2)}) %collective-permute-start.2) | collective-permute-done | bytes 860192 | tf_op jit(solution)/shard_map/ppermute | solution.py:43
  64.3 5.9 %collective-permute-done.3.refs_3_ = bf16[1680,256]{1,0:T(8,128)(2,1)} collective-permute-done((bf16[1680,256]{1,0:T(8,128)(2,1)}, bf16[1680,256]{1,0:T(8,128)(2,1)}, u32[]{:S(2)}, u32[]{:S(2)}) %collective-permute-start.3) | collective-permute-done | bytes 860192 | tf_op jit(solution)/shard_map/ppermute | solution.py:43
  70.2 0.0 slice-done.2
  70.2 0.0 copy-done.2
  70.2 7.0 %cross_last.1 = f32[6,11,256,256]{3,2,1,0:T(8,128)} custom-call(s32[6,11]{1,0:T(8,128)} %mask_hbm.5, s32[6]{0:T(128)} %branch_hbm.5, bf16[6,11,256,256]{3,2,1,0:T(8,128)(2,1)S(1)} %bitcast.7, f32[6,11,256,256]{3,2,1,0:T(8,128)} %get-tuple-element.21._, f32[15,256,256]{2,1,0:T(8,128)S(1)} %copy-done.2, ...), custom_call_target="tpu_custom_call", output_to_operand_aliasing={{}: (3, {})} | custom-call | flops 3690987520 | bytes 12582912 | tf_op jit(solution)/shard_map/cross_last/pallas_call | solution.py:491
  77.2 0.0 collective-permute-done.6
  77.2 0.0 collective-permute-done.5
  77.2 0.0 collective-permute-done.4
  77.3 0.5 multiply_bitcast_fusion
  (8 shorter events, 0.0 us)
Async XLA Ops:
  0.6 9.0 %copy-start = (bf16[6,11,256,256]{3,2,1,0:T(8,128)(2,1)S(1)}, bf16[6,11,256,256]{3,2,1,0:T(8,128)(2,1)}, u32[]{:S(2)}) copy-start(bf16[6,11,256,256]{3,2,1,0:T(8,128)(2,1)} %tiles_ref.7) | copy-start | bytes 25952260
  2.7 20.9 %collective-permute-start = (bf16[1680,256]{1,0:T(8,128)(2,1)S(1)}, bf16[1680,256]{1,0:T(8,128)(2,1)S(1)}, u32[]{:S(2)}, u32[]{:S(2)}) collective-permute-start(bf16[1680,256]{1,0:T(8,128)(2,1)S(1)} %get-tuple-element.15), channel_id=1, source_target_pairs={{0,1},{1,0},{2,3},{3,2},{4,5},{5,4},{6,7},{7,6},{8,9},{9,8},{10,11... | collective-permute-start | bytes 2580488 | tf_op jit(solution)/shard_map/ppermute | solution.py:43
  4.3 26.2 %collective-permute-start.1 = (bf16[1680,256]{1,0:T(8,128)(2,1)S(1)}, bf16[1680,256]{1,0:T(8,128)(2,1)S(1)}, u32[]{:S(2)}, u32[]{:S(2)}) collective-permute-start(bf16[1680,256]{1,0:T(8,128)(2,1)S(1)} %get-tuple-element.16), channel_id=1, source_target_pairs={{1,2},{2,1},{3,4},{4,3},{5,6},{6,5},{7,8},{8,7},{9,10},{10,9},{11,... | collective-permute-start | bytes 2580488 | tf_op jit(solution)/shard_map/ppermute | solution.py:43
  20.8 13.9 %copy-start.3 = (bf16[1680,256]{1,0:T(8,128)(2,1)}, bf16[1680,256]{1,0:T(8,128)(2,1)S(1)}, u32[]{:S(2)}) copy-start(bf16[1680,256]{1,0:T(8,128)(2,1)S(1)} %get-tuple-element.26) | copy-start | bytes 2580484
  20.8 15.8 %copy-start.4 = (bf16[1680,256]{1,0:T(8,128)(2,1)}, bf16[1680,256]{1,0:T(8,128)(2,1)S(1)}, u32[]{:S(2)}) copy-start(bf16[1680,256]{1,0:T(8,128)(2,1)S(1)} %get-tuple-element.25) | copy-start | bytes 2580484
  30.6 39.6 %slice-start = ((s8[8650752]{0:T(1024)(128)(4,1)}), s8[262144]{0:T(1024)(128)(4,1)S(1)}, s32[]{:S(2)}) async-start(s8[8650752]{0:T(1024)(128)(4,1)} %bitcast.6), calls=%async_computation.1 | async-start | bytes 524288
  34.7 1.9 %copy-start.1 = (f32[15,256,256]{2,1,0:T(8,128)}, f32[15,256,256]{2,1,0:T(8,128)S(1)}, u32[]{:S(2)}) copy-start(f32[15,256,256]{2,1,0:T(8,128)S(1)} %get-tuple-element.22.ready_ref) | copy-start | bytes 11796484
  36.6 12.5 %all-to-all-start = ((f32[32,1,128]{2,1,0:T(1,128)}), f32[32,1,128]{2,1,0:T(1,128)S(1)}, u32[]{:S(2)}, u32[]{:S(2)}) async-start(f32[32,1,128]{2,1,0:T(1,128)} %bitcast.1), calls=%async_computation | async-start | bytes 32768 | tf_op jit(solution)/shard_map/all_to_all | solution.py:542
  42.8 21.4 %collective-permute-start.2 = (bf16[1680,256]{1,0:T(8,128)(2,1)}, bf16[1680,256]{1,0:T(8,128)(2,1)S(1)}, u32[]{:S(2)}, u32[]{:S(2)}) collective-permute-start(bf16[1680,256]{1,0:T(8,128)(2,1)} %copy-done.4), channel_id=1, source_target_pairs={{0,1},{1,0},{2,3},{3,2},{4,5},{5,4},{6,7},{7,6},{8,9},{9,8},{10,11... | collective-permute-start | bytes 2580488 | tf_op jit(solution)/shard_map/ppermute | solution.py:43
  42.9 27.3 %collective-permute-start.3 = (bf16[1680,256]{1,0:T(8,128)(2,1)}, bf16[1680,256]{1,0:T(8,128)(2,1)}, u32[]{:S(2)}, u32[]{:S(2)}) collective-permute-start(bf16[1680,256]{1,0:T(8,128)(2,1)} %copy-done.3), channel_id=1, source_target_pairs={{1,2},{2,1},{3,4},{4,3},{5,6},{6,5},{7,8},{8,7},{9,10},{10,9},{11,... | collective-permute-start | bytes 2580488 | tf_op jit(solution)/shard_map/ppermute | solution.py:43
  49.1 21.1 %slice-start.1 = ((s8[8650752]{0:T(1024)(128)(4,1)}), s8[4194304]{0:T(1024)(128)(4,1)S(1)}, s32[]{:S(2)}) async-start(s8[8650752]{0:T(1024)(128)(4,1)} %bitcast.6), calls=%async_computation.2 | async-start | bytes 8388608
  49.1 21.1 %slice-start.2 = ((s8[8650752]{0:T(1024)(128)(4,1)}), s8[4194304]{0:T(1024)(128)(4,1)S(1)}, s32[]{:S(2)}) async-start(s8[8650752]{0:T(1024)(128)(4,1)} %bitcast.6), calls=%async_computation.3 | async-start | bytes 8388608
  49.1 21.1 %copy-start.2 = (f32[15,256,256]{2,1,0:T(8,128)S(1)}, f32[15,256,256]{2,1,0:T(8,128)}, u32[]{:S(2)}) copy-start(f32[15,256,256]{2,1,0:T(8,128)} %copy-done.1) | copy-start | bytes 11796484
  49.1 28.1 %collective-permute-start.6 = (f32[1,128]{1,0:T(1,128)S(1)}, f32[1,128]{1,0:T(1,128)S(1)}, u32[]{:S(2)}, u32[]{:S(2)}) collective-permute-start(f32[1,128]{1,0:T(1,128)S(1)} %add_rows.1), channel_id=1, source_target_pairs={{0,3},{1,2},{2,1},{3,0},{4,7},{5,6},{6,5},{7,4},{8,11},{9,10},{10,... | collective-permute-start | bytes 1544 | tf_op jit(solution)/shard_map/ppermute | solution.py:545
  51.5 25.7 %collective-permute-start.5 = (f32[1,128]{1,0:T(1,128)S(1)}, f32[1,128]{1,0:T(1,128)S(1)}, u32[]{:S(2)}, u32[]{:S(2)}) collective-permute-start(f32[1,128]{1,0:T(1,128)S(1)} %add_rows.1), channel_id=1, source_target_pairs={{0,2},{1,3},{2,0},{3,1},{4,6},{5,7},{6,4},{7,5},{8,10},{9,11},{10,... | collective-permute-start | bytes 1544 | tf_op jit(solution)/shard_map/ppermute | solution.py:545
  51.5 25.7 %collective-permute-start.4 = (f32[1,128]{1,0:T(1,128)S(1)}, f32[1,128]{1,0:T(1,128)S(1)}, u32[]{:S(2)}, u32[]{:S(2)}) collective-permute-start(f32[1,128]{1,0:T(1,128)S(1)} %add_rows.1), channel_id=1, source_target_pairs={{0,1},{1,0},{2,3},{3,2},{4,5},{5,4},{6,7},{7,6},{8,9},{9,8},{10,11... | collective-permute-start | bytes 1544 | tf_op jit(solution)/shard_map/ppermute | solution.py:545
